TPU v7x, 8 devices: a whole 2x2x1 slice. The times are simulated.
8 devices in a mesh: dp: 1 (over z), ffn: 2 (over y), emb: 4 (over x, core).
Axes of the slice: x: 2, y: 2, z: 1, core: 2. Of those that a mesh axis runs over, the one named last changes fastest.
Arguments:
- hidden: bfloat16 [128, 2048], P('dp', 'emb')
- norm_pre: bfloat16 [2048], P('emb')
- norm_post: bfloat16 [2048], P('emb')
- w_router: bfloat16 [2048, 64], P('emb')
- w_gate: bfloat16 [64, 2048, 1024], P(None, 'emb', 'ffn')
- w_up: bfloat16 [64, 2048, 1024], P(None, 'emb', 'ffn')
- w_down: bfloat16 [64, 1024, 2048], P(None, 'ffn', 'emb')
- choice: int32 [128, 8], P('dp')
Outputs:
- output: bfloat16 [128, 2048], P('dp', 'emb')
All inputs are finite; a program needn't handle non-finite values.
Results may differ from a plain program's by a relative error of at most 0.0126077.
Values are sent between devices in bfloat16 or wider.
A program may use at most 1 GiB of HBM per device.

v0:
```python
import jax
import jax.numpy as jnp
from jax import lax
from jax.sharding import PartitionSpec as P

EPS = 1e-5


def route_tokens(choice, router_prob, experts, capacity):
    num_tok, top_k = choice.shape
    onehot = (choice[:, :, None] == jnp.arange(experts)[None, None, :]).astype(jnp.int32)
    assigned = jnp.sum(onehot, axis=1)
    before = jnp.cumsum(assigned, axis=0) - assigned
    slot_idx = jnp.sum(onehot * before[:, None, :], axis=2)
    position = jnp.where(slot_idx < capacity, choice * capacity + slot_idx, experts * capacity)
    gate_val = jnp.take_along_axis(router_prob, choice, axis=1)
    flat_pos = position.reshape(-1)
    token_ids = jnp.repeat(jnp.arange(num_tok, dtype=jnp.int32), top_k)
    slot_token = jnp.full((experts * capacity,), num_tok, jnp.int32).at[flat_pos].set(token_ids, mode='drop')
    slot_gate = jnp.zeros((experts * capacity,), jnp.float32).at[flat_pos].set(gate_val.reshape(-1), mode='drop')
    return position, slot_token, slot_gate


def solution(mesh):
    emb_size = mesh.shape['emb']

    def local_block(hidden, norm_pre, norm_post, w_router, w_gate, w_up, w_down, choice):
        num_tok, local_width = hidden.shape
        model_width = local_width * emb_size
        experts = w_gate.shape[0]
        top_k = choice.shape[1]
        capacity = 2 * num_tok * top_k // experts
        hid_f32 = hidden.astype(jnp.float32)
        sq_pre = lax.psum(jnp.sum(hid_f32 * hid_f32, axis=1, keepdims=True), 'emb')
        inv_pre = lax.rsqrt(sq_pre / model_width + EPS)
        normed = (hid_f32 * inv_pre * norm_pre.astype(jnp.float32)).astype(jnp.bfloat16)
        logits = lax.psum(jnp.dot(normed, w_router, preferred_element_type=jnp.float32), 'emb')
        router_prob = jax.nn.softmax(logits, axis=1)
        position, slot_token, slot_gate = route_tokens(choice, router_prob, experts, capacity)
        expert_in = jnp.take(normed, slot_token, axis=0, mode='fill', fill_value=0).reshape(experts, capacity, local_width)
        z_gate = jnp.einsum('ecd,edf->ecf', expert_in, w_gate, preferred_element_type=jnp.float32).astype(jnp.bfloat16)
        z_up = jnp.einsum('ecd,edf->ecf', expert_in, w_up, preferred_element_type=jnp.float32).astype(jnp.bfloat16)
        z_gate, z_up = lax.psum((z_gate, z_up), 'emb')
        act_val = (jax.nn.gelu(z_gate.astype(jnp.float32), approximate=True) * z_up.astype(jnp.float32)).astype(jnp.bfloat16)
        part_out = jnp.einsum('ecf,efd->ecd', act_val, w_down, preferred_element_type=jnp.float32).astype(jnp.bfloat16)
        expert_out = lax.psum(part_out, 'ffn')
        weighted = (expert_out.reshape(experts * capacity, local_width).astype(jnp.float32) * slot_gate[:, None]).astype(jnp.bfloat16)
        picked = jnp.take(weighted, position, axis=0, mode='fill', fill_value=0)
        mix_sum = jnp.sum(picked.astype(jnp.float32), axis=1)
        sq_post = lax.psum(jnp.sum(mix_sum * mix_sum, axis=1, keepdims=True), 'emb')
        inv_post = lax.rsqrt(sq_post / model_width + EPS)
        return (hid_f32 + mix_sum * inv_post * norm_post.astype(jnp.float32)).astype(jnp.bfloat16)

    in_specs = (P('dp', 'emb'), P('emb'), P('emb'), P('emb', None), P(None, 'emb', 'ffn'), P(None, 'emb', 'ffn'), P(None, 'ffn', 'emb'), P('dp', None))
    return jax.shard_map(local_block, mesh=mesh, in_specs=in_specs, out_specs=P('dp', 'emb'), check_vma=False)
```

profile of v0, /device:TPU:0, one launch (start us, length us, event | category | flops | bytes accessed | tf_op | source)
XLA Modules:
  0.0 239.5 jit_solution(8892392327661447181)
XLA Ops:
  6.5 0.8 convert_reduce_fusion.1
  7.4 0.2 reduce_window_sum.11
  7.6 0.7 select_reduce_fusion
  8.4 0.7 compare_and_fusion.1
  9.4 4.3 %scatter_custom_fusion = s32[2048]{0:T(1024)S(1)} fusion(s32[1024]{0:T(1024)S(1)} %bitcast.27, s32[1024]{0:T(1024)S(1)} %reshape.112, s32[]{:T(128)} %constant.34.clone.1), kind=kCustom, calls=%fused_computation.53 | custom fusion | bytes 8196 | tf_op jit(solution)/shard_map/scatter | solution.py:19
  13.8 1.0 fusion.18
  14.8 8.8 %psum.42 = f32[128,1]{0,1:T(1,128)S(1)} all-reduce(f32[128,1]{0,1:T(1,128)S(1)} %bitcast.29), channel_id=1, replica_groups=mesh['dp'=1,'ffn'=2,'emb'=4] {'emb'}, use_global_device_ids=true, to_apply=%region_5.0 | all-reduce | flops 128 | bytes 1024 | tf_op jit(solution)/shard_map/psum | solution.py:34
  23.5 0.7 convert_element_type.50
  24.3 1.0 fusion.20
  25.3 7.5 %gather_fusion = bf16[2048,512]{1,0:T(8,128)(2,1)S(1)} fusion(bf16[128,512]{1,0:T(8,128)(2,1)S(1)} %fusion.20, s32[2048]{0:T(1024)S(1)} %fusion.24), kind=kCustom, calls=%fused_computation | custom fusion | bytes 4202496 | tf_op jit(solution)/shard_map/jit(_take)/gather | solution.py:40
  32.9 15.0 %convolution_convert_fusion = bf16[64,32,512]{2,1,0:T(8,128)(2,1)} fusion(bf16[64,512,512]{2,1,0:T(8,128)(2,1)} %param.13, bf16[64,32,512]{2,1,0:T(8,128)(2,1)S(1)} %bitcast.24, pred[64,32]{1,0:T(8,128)(4,1)S(1)} %broadcast_in_dim.63), kind=kOutput, calls=%fused_computation.24 | convolution fusion | flops 1075838976 | bytes 37750784 | tf_op jit(solution)/shard_map/ecd,edf->ecf/dot_general | solution.py:42
  47.8 15.0 %convolution_convert_fusion.1 = bf16[64,32,512]{2,1,0:T(8,128)(2,1)} fusion(bf16[64,512,512]{2,1,0:T(8,128)(2,1)} %param.12, bf16[64,32,512]{2,1,0:T(8,128)(2,1)S(1)} %bitcast.25, pred[64,32]{1,0:T(8,128)(4,1)S(1)} %broadcast_in_dim.63), kind=kOutput, calls=%fused_computation.25 | convolution fusion | flops 1075838976 | bytes 37750784 | tf_op jit(solution)/shard_map/ecd,edf->ecf/dot_general | solution.py:41
  62.9 79.9 %all-reduce.6.cloned.1.call-done = (bf16[64,32,512]{2,1,0:T(8,128)(2,1)}, bf16[64,32,512]{2,1,0:T(8,128)(2,1)}) async-done(((bf16[64,32,512]{2,1,0:T(8,128)(2,1)}, bf16[64,32,512]{2,1,0:T(8,128)(2,1)}), (bf16[64,32,512]{2,1,0:T(8,128)(2,1)}, bf16[64,32,512]{2,1,0:T(8,128)(2,1)})) %all-reduce.6.cloned.1.call-update) | async-done | bytes 4194320 | tf_op jit(solution)/shard_map/psum | solution.py:43
  142.8 18.4 %fusion.13 = bf16[64,32,512]{2,1,0:T(8,128)(2,1)} fusion(bf16[64,512,512]{2,1,0:T(8,128)(2,1)} %param.14, bf16[64,32,512]{2,1,0:T(8,128)(2,1)} %get-tuple-element.5, bf16[64,32,512]{2,1,0:T(8,128)(2,1)} %get-tuple-element.6), kind=kOutput, calls=%fused_computation.26 | convolution fusion | flops 1087373312 | bytes 39845888 | tf_op jit(solution)/shard_map/ecf,efd->ecd/dot_general | solution.py:45
  161.8 0.2 fusion.35
  162.0 10.8 %psum.46 = f32[128,64]{0,1:T(8,128)S(1)} all-reduce(f32[128,64]{0,1:T(8,128)S(1)} %fusion.35), channel_id=1, replica_groups=mesh['dp'=1,'ffn'=2,'emb'=4] {'emb'}, use_global_device_ids=true, to_apply=%region_9.10 | all-reduce | flops 8192 | bytes 65536 | tf_op jit(solution)/shard_map/psum | solution.py:37
  172.9 7.0 %gather_fusion.2 = f32[1024]{0:T(1024)S(1)} fusion(f32[128,64]{0,1:T(8,128)S(1)} %fusion.22, s32[1024]{0:T(1024)S(1)} %reshape.102), kind=kCustom, calls=%fused_computation.2 | custom fusion | bytes 16384 | tf_op jit(solution)/shard_map/jit(take_along_axis)/gather | solution.py:16
  180.3 4.3 %scatter_custom_fusion.1 = f32[2048]{0:T(1024)S(1)} fusion(s32[1024]{0:T(1024)S(1)} %bitcast.28, f32[1024]{0:T(1024)S(1)} %reshape.120, f32[]{:T(128)} %constant.42.clone.1), kind=kCustom, calls=%fused_computation.51 | custom fusion | bytes 8196 | tf_op jit(solution)/shard_map/scatter | solution.py:20
  184.7 34.1 %all-reduce.4.cloned.1.call-done = bf16[2048,512]{1,0:T(8,128)(2,1)} async-done(((bf16[2048,512]{1,0:T(8,128)(2,1)}), bf16[2048,512]{1,0:T(8,128)(2,1)}) %all-reduce.4.cloned.1.call-update) | async-done | bytes 2097168 | tf_op jit(solution)/shard_map/psum | solution.py:46
  218.7 2.0 multiply_convert_fusion
  220.8 4.0 %gather_fusion.1 = bf16[1024,512]{1,0:T(8,128)(2,1)S(1)} fusion(bf16[2048,512]{1,0:T(8,128)(2,1)S(1)} %multiply_convert_fusion, s32[1024]{0:T(1024)S(1)} %broadcast_clamp_fusion), kind=kCustom, calls=%fused_computation.1 | custom fusion | bytes 2101248 | tf_op jit(solution)/shard_map/jit(_take)/gather | solution.py:48
  224.8 0.7 convert_reduce_fusion
  225.6 6.3 %psum.47 = f32[128,1]{0,1:T(1,128)S(1)} all-reduce(f32[128,1]{0,1:T(1,128)S(1)} %bitcast.30), channel_id=1, replica_groups=mesh['dp'=1,'ffn'=2,'emb'=4] {'emb'}, use_global_device_ids=true, to_apply=%region_15.16 | all-reduce | flops 128 | bytes 1024 | tf_op jit(solution)/shard_map/psum | solution.py:50
  231.9 0.8 fusion.21
  (43 shorter events, 1.7 us)
Async XLA Ops:
  6.5 155.3 %copy-start = (bf16[512,64]{0,1:T(8,128)(2,1)S(1)}, bf16[512,64]{0,1:T(8,128)(2,1)}, u32[]{:S(2)}) copy-start(bf16[512,64]{0,1:T(8,128)(2,1)} %param.11) | copy-start | bytes 196612
  6.5 136.3 %all-reduce.6.cloned.1.call-start = ((), (), s32[]{:S(2)}) async-start(), calls=%async_computation.1 | async-start | bytes 8388608 | tf_op jit(solution)/shard_map/psum | solution.py:43
  62.9 155.9 %all-reduce.4.cloned.1.call-start = ((), (), s32[]{:S(2)}) async-start(), calls=%async_computation | async-start | bytes 4194304 | tf_op jit(solution)/shard_map/psum | solution.py:46
  142.8 18.4 %copy-start.3 = (bf16[512]{0:T(512)(128)(2,1)S(1)}, bf16[512]{0:T(512)(128)(2,1)}, u32[]{:S(2)}) copy-start(bf16[512]{0:T(512)(128)(2,1)} %param.10) | copy-start | bytes 3076
  142.8 18.5 %copy-start.2 = (s32[128,8]{0,1:T(8,128)S(1)}, s32[128,8]{0,1:T(8,128)}, u32[]{:S(2)}) copy-start(s32[128,8]{0,1:T(8,128)} %param.15) | copy-start | bytes 12292
  220.8 11.1 %copy-start.1 = (bf16[128,512]{1,0:T(8,128)(2,1)S(1)}, bf16[128,512]{1,0:T(8,128)(2,1)}, u32[]{:S(2)}) copy-start(bf16[128,512]{1,0:T(8,128)(2,1)} %param.8) | copy-start | bytes 393220
Sparse Core Ops, SparseCore 0:
  63.0 79.7 all-reduce.5
  161.4 57.3 all-reduce.3
where the time goes:
time: 240 us
  waiting for transfers between devices  114 us (48%)
  matrix products  48.5 us (20%)
  local copies, waits for them, and re-layouts  28.6 us (12%)
  blocking collectives  25.9 us (11%)
  between operations  13.6 us (6%)
  other arithmetic  8.84 us (4%)
    psum x1, waiting for transfers between devices, local_block(): z_gate, z_up = lax.psum((z_gate, z_up), 'emb')  79.9 us
    psum x1, waiting for transfers between devices, local_block(): expert_out = lax.psum(part_out, 'ffn')  34.1 us
    dot_general x1, matrix products, local_block(): jnp.einsum('ecf,efd->ecd', act_val, w_down, preferred_element_type=jnp.fl...  18.4 us
    dot_general x1, matrix products, local_block(): jnp.einsum('ecd,edf->ecf', expert_in, w_gate, preferred_element_type=jnp....  15 us
    dot_general x1, matrix products, local_block(): jnp.einsum('ecd,edf->ecf', expert_in, w_up, preferred_element_type=jnp.fl...  15 us
    psum x1, blocking collectives, local_block(): lax.psum(jnp.dot(normed, w_router, preferred_element_type=jnp.float32), '...  10.8 us
    psum x1, blocking collectives, local_block(): sq_pre = lax.psum(jnp.sum(hid_f32 * hid_f32, axis=1, keepdims=True), 'emb')  8.75 us
    gather x1, local copies, waits for them, and re-layouts, local_block(): jnp.take(normed, slot_token, axis=0, mode='fill', fill_value=0)  7.54 us
  transfers between devices with their start and end apart: 2, of which 2 were waited for; matrix products, arithmetic and copies ran while one was open for 5% of the time, Pallas kernels for 0%

commit v1 on v0

v1 whole, which is shorter than its diff:
```python
import functools

import jax
import jax.numpy as jnp
from jax import lax
from jax.experimental import pallas as pl
from jax.experimental.pallas import tpu as pltpu
from jax.sharding import PartitionSpec as P

EPS = 1e-5
MESH = pl.DeviceIdType.MESH
F32 = jnp.float32
BF16 = jnp.bfloat16

CE = 4
NB = 6
NC = 8
LAG_B, LAG_C, LAG_D, LAG_E = 1, 3, 5, 6


def kernel(tok, wid, experts, cap, width, top_k, model_width,
           hid_hbm, pre_ref, post_ref, wr_hbm, wg_hbm, wu_hbm, wd_hbm, ch_hbm, out_ref,
           hid, wr, ch, wg, wu, wd, key, xs, sel, gate, zbuf, rza, sbuf, rzb, gbuf, mix, rmix,
           sqs, sqr, lgs, lgr, sqs2, sqr2,
           small_sem, wg_sem, wu_sem, wd_sem,
           as_sem, ar_sem, bs_sem, br_sem, gcs_sem, gcr_sem, gxs_sem, gxr_sem, gfs_sem, gfr_sem,
           ss_sem, sr_sem, ls_sem, lr_sem, ps_sem, pr_sem, ms_sem, mr_sem):
    nchunk = experts // CE
    rows = CE * cap
    emb = lax.axis_index("emb")
    ffn = lax.axis_index("ffn")
    x, c = emb // 2, emb % 2
    ox, oc = 1 - x, 1 - c
    mate = {"emb": x * 2 + oc}
    across = {"emb": ox * 2 + c}
    diag = {"emb": ox * 2 + oc}
    other = {"ffn": 1 - ffn}
    peers = (mate, across, diag)

    def weight_copies(i):
        s = lax.rem(i, NB)
        e = pl.ds(i * CE, CE)
        return (pltpu.make_async_copy(wg_hbm.at[e], wg.at[s], wg_sem.at[s]),
                pltpu.make_async_copy(wu_hbm.at[e], wu.at[s], wu_sem.at[s]))

    def down_copy(i):
        s = lax.rem(i, NC)
        return pltpu.make_async_copy(wd_hbm.at[pl.ds(i * CE, CE)], wd.at[s], wd_sem.at[s])

    small = (pltpu.make_async_copy(hid_hbm, hid, small_sem.at[0]),
             pltpu.make_async_copy(ch_hbm, ch, small_sem.at[1]),
             pltpu.make_async_copy(wr_hbm, wr, small_sem.at[2]))
    for cp in small:
        cp.start()
    for i in range(NB):
        for cp in weight_copies(i):
            cp.start()

    barrier = pltpu.get_barrier_semaphore()
    for peer in peers + (other,):
        pl.semaphore_signal(barrier, inc=1, device_id=peer, device_id_type=MESH)

    def gather_small(src, dst, send, recv):
        cps = [pltpu.make_async_remote_copy(src, dst.at[j], send.at[j], recv.at[j], device_id=peer, device_id_type=MESH)
               for j, peer in enumerate(peers)]
        for cp in cps:
            cp.start()
        return cps

    def row_sums(sq):
        part = sq[:, 0:128]
        for j in range(1, width // 128):
            part = part + sq[:, j * 128:(j + 1) * 128]
        t = jnp.sum(part.T, axis=0, keepdims=True)
        return jnp.broadcast_to(t, (8, tok))

    def as_row(ref):
        v = ref[...].astype(F32)
        return jnp.concatenate([v[j:j + 1, :] for j in range(width // 128)], axis=1)

    small[0].wait()
    hf = hid[...].astype(F32)
    sqs[...] = row_sums(hf * hf)
    pl.semaphore_wait(barrier, 4)
    sq_cps = gather_small(sqs, sqr, ss_sem, sr_sem)

    small[1].wait()
    expert_id = lax.broadcasted_iota(jnp.int32, (experts, tok), 0)
    chv = ch[...]
    hot = jnp.zeros((experts, tok), F32)
    for k in range(top_k):
        hot = hot + jnp.where(chv[k:k + 1, :] == expert_id, 1.0, 0.0)
    t0 = lax.broadcasted_iota(jnp.int32, (tok, tok), 0)
    t1 = lax.broadcasted_iota(jnp.int32, (tok, tok), 1)
    upper = jnp.where(t0 < t1, 1.0, 0.0).astype(BF16)
    before = jnp.dot(hot.astype(BF16), upper, preferred_element_type=F32)
    key_val = jnp.where((hot > 0.5) & (before < cap - 0.5), before, -1.0)
    dn = (((0,), (0,)), ((), ()))
    slot = lax.broadcasted_iota(jnp.int32, (cap, tok), 0).astype(F32)
    for e in range(experts):
        sel[e * cap:(e + 1) * cap, :] = jnp.where(key_val[e:e + 1, :] == slot, 1.0, 0.0).astype(BF16)

    for cp in sq_cps:
        cp.wait_recv()
    tot = (sqs[0:1, :] + sqr[0, 0:1, :]) + (sqr[1, 0:1, :] + sqr[2, 0:1, :])
    inv = lax.rsqrt(tot / model_width + EPS)
    inv = jnp.broadcast_to(inv, (tok, tok)).T
    inv = jnp.concatenate([inv] * (width // 128), axis=1)
    b = (hf * inv * as_row(pre_ref)).astype(BF16)
    small[2].wait()
    lgs[...] = lax.dot_general(wr[...], b, (((1,), (1,)), ((), ())), preferred_element_type=F32)
    lg_cps = gather_small(lgs, lgr, ls_sem, lr_sem)
    for r in range(0, experts * cap, 256):
        xs[r:r + 256, :] = jnp.dot(sel[r:r + 256, :], b, preferred_element_type=F32).astype(BF16)
    mix[...] = jnp.zeros_like(mix)

    def gates():
        for cp in lg_cps:
            cp.wait_recv()
        lg = (lgs[...] + lgr[0]) + (lgr[1] + lgr[2])
        lg = lg - jnp.max(lg, axis=0, keepdims=True)
        ex = jnp.exp(lg)
        prob = ex / jnp.sum(ex, axis=0, keepdims=True)
        for e in range(experts):
            picked = jnp.where(key_val[e:e + 1, :] == slot, prob[e:e + 1, :], 0.0)
            gate[e * cap:(e + 1) * cap, :] = jnp.broadcast_to(jnp.sum(picked, axis=1, keepdims=True), (cap, 128))

    gates()

    def send_z(i):
        return pltpu.make_async_remote_copy(zbuf.at[i, oc], rza.at[i], as_sem.at[i], ar_sem.at[i],
                                            device_id=mate, device_id_type=MESH)

    def send_s(i):
        return pltpu.make_async_remote_copy(sbuf.at[i], rzb.at[i], bs_sem.at[i], br_sem.at[i],
                                            device_id=across, device_id_type=MESH)

    def send_g(i):
        own = gbuf.at[i, c, x]
        return (pltpu.make_async_remote_copy(own, own, gcs_sem.at[i], gcr_sem.at[i],
                                             device_id=mate, device_id_type=MESH),
                pltpu.make_async_remote_copy(own, own, gxs_sem.at[i], gxr_sem.at[i],
                                             device_id=across, device_id_type=MESH))

    def recv_mate(i):
        z = gbuf.at[i, oc, x]
        return pltpu.make_async_remote_copy(z, z, gcs_sem.at[i], gcr_sem.at[i], device_id=mate, device_id_type=MESH)

    def recv_across(i):
        z = gbuf.at[i, c, ox]
        return pltpu.make_async_remote_copy(z, z, gxs_sem.at[i], gxr_sem.at[i], device_id=across, device_id_type=MESH)

    def forward_g(i):
        z = gbuf.at[i, c, ox]
        return pltpu.make_async_remote_copy(z, z, gfs_sem.at[i], gfr_sem.at[i], device_id=mate, device_id_type=MESH)

    def arrived_g(i):
        z = gbuf.at[i, oc, ox]
        return pltpu.make_async_remote_copy(z, z, gfs_sem.at[i], gfr_sem.at[i], device_id=mate, device_id_type=MESH)

    def stage_a(i):
        s = lax.rem(i, NB)
        for cp in weight_copies(i):
            cp.wait()
        base = pl.multiple_of(i * rows, rows)
        for k in range(CE):
            xe = xs[pl.ds(base + k * cap, cap), :]
            zbuf[i, k // 2, k % 2, :, 0:width] = jnp.dot(xe, wg[s, k], preferred_element_type=F32).astype(BF16)
            zbuf[i, k // 2, k % 2, :, width:2 * width] = jnp.dot(xe, wu[s, k], preferred_element_type=F32).astype(BF16)
        send_z(i).start()

    def refill(i):
        for cp in weight_copies(i):
            cp.start()

    def stage_b(i):
        send_z(i).wait_recv()
        sbuf[i] = (zbuf[i, c, ox].astype(F32) + rza[i, ox].astype(F32)).astype(BF16)
        send_s(i).start()

    def stage_c(i):
        send_s(i).wait_recv()
        z = (zbuf[i, c, x].astype(F32) + rza[i, x].astype(F32) + rzb[i].astype(F32)).astype(BF16).astype(F32)
        act = jax.nn.gelu(z[:, 0:width], approximate=True) * z[:, width:2 * width]
        gbuf[i, c, x] = act.astype(BF16)
        for cp in send_g(i):
            cp.start()

    def stage_d(i):
        recv_across(i).wait_recv()
        forward_g(i).start()

    def stage_e(i):
        s = lax.rem(i, NC)
        down_copy(i).wait()
        recv_mate(i).wait_recv()
        arrived_g(i).wait_recv()
        base = pl.multiple_of(i * rows, rows)
        us = []
        for k in range(CE):
            y = jnp.dot(gbuf[i, k // 2, k % 2], wd[s, k], preferred_element_type=F32).astype(BF16).astype(F32)
            gk = gate[pl.ds(base + k * cap, cap), :]
            us.append((y * jnp.concatenate([gk] * (width // 128), axis=1)).astype(BF16))
        u = jnp.concatenate(us, axis=0)
        mix[...] += lax.dot_general(sel[pl.ds(base, rows), :], u, dn, preferred_element_type=F32)

    def guarded(i):
        pl.when(i >= LAG_B)(lambda: stage_b(i - LAG_B))
        pl.when(i >= LAG_C)(lambda: stage_c(i - LAG_C))
        pl.when(i >= LAG_D)(lambda: stage_d(i - LAG_D))

    @pl.loop(0, LAG_E)
    def _(i):
        down_copy(i).start()
        stage_a(i)
        refill(i + NB)
        guarded(i)

    @pl.loop(LAG_E, nchunk)
    def _(i):
        down_copy(i).start()
        stage_a(i)
        pl.when(i + NB < nchunk)(lambda: refill(i + NB))
        stage_b(i - LAG_B)
        stage_c(i - LAG_C)
        stage_d(i - LAG_D)
        stage_e(i - LAG_E)

    @pl.loop(nchunk, nchunk + LAG_E)
    def _(i):
        pl.when(i - LAG_B < nchunk)(lambda: stage_b(i - LAG_B))
        pl.when(i - LAG_C < nchunk)(lambda: stage_c(i - LAG_C))
        pl.when(i - LAG_D < nchunk)(lambda: stage_d(i - LAG_D))
        stage_e(i - LAG_E)

    mcp = pltpu.make_async_remote_copy(mix, rmix, ms_sem, mr_sem, device_id=other, device_id_type=MESH)
    mcp.start()

    @pl.loop(0, nchunk)
    def _(i):
        send_z(i).wait_send()
        send_s(i).wait_send()
        for cp in send_g(i):
            cp.wait_send()
        forward_g(i).wait_send()

    for cp in sq_cps + lg_cps:
        cp.wait_send()
    mcp.wait()
    m = mix[...] + rmix[...]
    sqs2[...] = row_sums(m * m)
    cps = gather_small(sqs2, sqr2, ps_sem, pr_sem)
    for cp in cps:
        cp.wait()
    tot = (sqs2[0:1, :] + sqr2[0, 0:1, :]) + (sqr2[1, 0:1, :] + sqr2[2, 0:1, :])
    inv = lax.rsqrt(tot / model_width + EPS)
    inv = jnp.broadcast_to(inv, (tok, tok)).T
    inv = jnp.concatenate([inv] * (width // 128), axis=1)
    out_ref[...] = (hid[...].astype(F32) + m * inv * as_row(post_ref)).astype(BF16)


def solution(mesh):
    emb_size = mesh.shape["emb"]

    def local_block(hidden, norm_pre, norm_post, w_router, w_gate, w_up, w_down, choice):
        tok, width = hidden.shape
        experts, _, wid = w_gate.shape
        top_k = choice.shape[1]
        cap = 2 * tok * top_k // experts
        nchunk = experts // CE
        dma = pltpu.SemaphoreType.DMA
        vmem = pltpu.VMEM
        assert emb_size == CE and wid == width
        hbm = pl.BlockSpec(memory_space=pl.ANY)
        vm = pl.BlockSpec(memory_space=pltpu.VMEM)
        return pl.pallas_call(
            functools.partial(kernel, tok, wid, experts, cap, width, top_k, width * emb_size),
            out_shape=jax.ShapeDtypeStruct((tok, width), BF16),
            in_specs=[hbm, vm, vm, hbm, hbm, hbm, hbm, hbm],
            out_specs=vm,
            scratch_shapes=[
                vmem((tok, width), BF16), vmem((experts, width), BF16), vmem((top_k, tok), jnp.int32),
                vmem((NB, CE, width, wid), BF16), vmem((NB, CE, width, wid), BF16), vmem((NC, CE, wid, width), BF16),
                vmem((8, 128), F32),
                vmem((experts * cap, width), BF16), vmem((experts * cap, tok), BF16), vmem((experts * cap, 128), F32),
                vmem((nchunk, 2, 2, cap, 2 * wid), BF16), vmem((nchunk, 2, cap, 2 * wid), BF16),
                vmem((nchunk, cap, 2 * wid), BF16), vmem((nchunk, cap, 2 * wid), BF16),
                vmem((nchunk, 2, 2, cap, wid), BF16),
                vmem((tok, width), F32), vmem((tok, width), F32),
                vmem((8, tok), F32), vmem((3, 8, tok), F32),
                vmem((experts, tok), F32), vmem((3, experts, tok), F32),
                vmem((8, tok), F32), vmem((3, 8, tok), F32),
                dma((3,)), dma((NB,)), dma((NB,)), dma((NC,)),
            ] + [dma((nchunk,))] * 10 + [dma((3,))] * 6 + [dma, dma],
            compiler_params=pltpu.CompilerParams(
                collective_id=0, has_side_effects=True, vmem_limit_bytes=67043328),
        )(hidden, norm_pre.reshape(width // 128, 128), norm_post.reshape(width // 128, 128), w_router.T, w_gate, w_up, w_down, choice.T)

    in_specs = (P("dp", "emb"), P("emb"), P("emb"), P("emb", None), P(None, "emb", "ffn"), P(None, "emb", "ffn"), P(None, "ffn", "emb"), P("dp", None))
    return jax.shard_map(local_block, mesh=mesh, in_specs=in_specs, out_specs=P("dp", "emb"), check_vma=False)
```

time: 240 us -> 69.8 us (0.29)
  waiting for transfers between devices: 114 us -> 0 us
  Pallas kernels: 0 us -> 68.1 us
  matrix products: 48.5 us -> 0 us
  local copies, waits for them, and re-layouts: 28.6 us -> 1.57 us
  blocking collectives: 25.9 us -> 0 us
  between operations: 13.6 us -> 0.01 us
  other arithmetic: 8.84 us -> 0 us
    psum x2 -> x0, waiting for transfers between devices: 114 us -> none  [the longest x1 79.9 us: local_block(): z_gate, z_up = lax.psum((z_gate, z_up), 'emb')]
    pallas_call x0 -> x1, Pallas kernels: none -> 68.1 us  [local_block(): pl.pallas_call(functools.partial(kernel, tok, wid, experts, cap, width, t...]
    dot_general x4 -> x0, matrix products: 48.5 us -> none  [the longest x1 18.4 us: local_block(): jnp.einsum('ecf,efd->ecd', act_val, w_down, preferred_element_type=jnp.fl...]
    psum x3 -> x0, blocking collectives: 25.9 us -> none  [the longest x1 10.8 us: local_block(): lax.psum(jnp.dot(normed, w_router, preferred_element_type=jnp.float32), '...]
    gather x7 -> x0, local copies, waits for them, and re-layouts: 18.9 us -> none  [the longest x1 7.54 us: local_block(): jnp.take(normed, slot_token, axis=0, mode='fill', fill_value=0)]
    scatter x2 -> x0, local copies, waits for them, and re-layouts: 8.63 us -> none  [the longest x1 4.32 us: route_tokens(): jnp.full((experts * capacity,), num_tok, jnp.int32).at[flat_pos]]
    convert_element_type x5 -> x0, other arithmetic: 4.5 us -> none  [the longest x1 2.04 us: local_block(): (expert_out.reshape(experts * capacity, local_width).astype(jnp.float32)...]
    reduce_sum x6 -> x0, other arithmetic: 3.36 us -> none  [the longest x1 1.01 us: local_block(): sq_pre = lax.psum(jnp.sum(hid_f32 * hid_f32, axis=1, keepdims=True), 'emb')]
  transfers between devices with their start and end apart: 2 -> 0, of which waited for: 2 -> 0; matrix products, arithmetic and copies ran while one was open for 5% -> 0% of each run, Pallas kernels for 0% -> 0%
where the time goes in v1:
time: 69.8 us; the launch traced here: 69.7 us
  Pallas kernels  68.1 us (98%)
  local copies, waits for them, and re-layouts  1.57 us (2%)
    pallas_call x1, Pallas kernels, local_block(): pl.pallas_call(functools.partial(kernel, tok, wid, experts, cap, width, t...  68.1 us
    unnamed x1, local copies, waits for them, and re-layouts  1.57 us

profile of v1, /device:TPU:0, one launch (start us, length us, event | category | flops | bytes accessed | tf_op | source)
XLA Modules:
  0.0 69.7 jit_solution(9528029754439670163)
XLA Ops:
  0.0 68.1 %shard_map.82 = bf16[128,512]{1,0:T(8,128)(2,1)} custom-call(bf16[128,512]{1,0:T(8,128)(2,1)} %hid_hbm.1, bf16[4,128]{1,0:T(4,128)(2,1)} %bitcast.6, bf16[4,128]{1,0:T(4,128)(2,1)} %bitcast.7, bf16[64,512]{1,0:T(8,128)(2,1)} %bitcast.4, bf16[64,512,512]{2,1,0:T(8,128)(2,1)} %wg_hbm.1, bf16[64,512,512]{2,1,0:T(8,128)(2,1)} %wu_hbm.1, ...), custom_call_target="tpu_custom_call" | custom-call | tf_op jit(solution)/shard_map/pallas_call | solution.py:276
  68.1 1.6 %copy.10 = bf16[128,512]{1,0:T(8,128)(2,1)} copy(bf16[128,512]{1,0:T(8,128)(2,1)} %shard_map.82) | data formatting | bytes 262144

commit v2 on v1

v2 whole, which is shorter than its diff:
```python
import functools

import jax
import jax.numpy as jnp
from jax import lax
from jax.experimental import pallas as pl
from jax.experimental.pallas import tpu as pltpu
from jax.sharding import PartitionSpec as P

EPS = 1e-5
MESH = pl.DeviceIdType.MESH
F32 = jnp.float32
BF16 = jnp.bfloat16

GE = 8
NP = 2
NR = 4


def kernel(tok, wid, experts, cap, width, top_k, model_width,
           hid_hbm, pre_ref, post_ref, wr_hbm, wg_hbm, wu_hbm, wd_hbm, ch_hbm, out_ref,
           hid, wr, ch, wg, wu, wd, xs, sel, dis, gate, zs, zc, rza, rzb, gbuf, mix, rmix,
           sqs, sqr, lgs, lgr, sqs2, sqr2,
           small_sem, wg_sem, wu_sem, wd_sem,
           as_sem, ar_sem, bs_sem, br_sem, gcs_sem, gcr_sem, gxs_sem, gxr_sem, gfs_sem, gfr_sem,
           ss_sem, sr_sem, ls_sem, lr_sem, ps_sem, pr_sem, ms_sem, mr_sem):
    groups = experts // GE
    half = groups // 2
    rows = GE * cap
    quarter = rows // 4
    fw = wid // NP
    emb = lax.axis_index("emb")
    ffn = lax.axis_index("ffn")
    x, c = emb // 2, emb % 2
    ox, oc = 1 - x, 1 - c
    mate = {"emb": x * 2 + oc}
    across = {"emb": ox * 2 + c}
    diag = {"emb": ox * 2 + oc}
    other = {"ffn": 1 - ffn}
    peers = (mate, across, diag)

    def weight_copies(p, g):
        e = pl.ds(g * GE, GE)
        col = pl.ds(p * fw, fw) if isinstance(p, int) else pl.ds(pl.multiple_of(p * fw, fw), fw)
        s = g % NR
        return (pltpu.make_async_copy(wg_hbm.at[e, :, col], wg.at[s], wg_sem.at[s]),
                pltpu.make_async_copy(wu_hbm.at[e, :, col], wu.at[s], wu_sem.at[s]))

    def down_copy(g):
        return pltpu.make_async_copy(wd_hbm.at[pl.ds(g * GE, GE)], wd.at[g], wd_sem.at[g])

    small = (pltpu.make_async_copy(hid_hbm, hid, small_sem.at[0]),
             pltpu.make_async_copy(ch_hbm, ch, small_sem.at[1]),
             pltpu.make_async_copy(wr_hbm, wr, small_sem.at[2]))
    for cp in small:
        cp.start()
    for g in range(NR):
        for cp in weight_copies(0, g):
            cp.start()
    down_copy(0).start()

    barrier = pltpu.get_barrier_semaphore()
    for peer in peers + (other,):
        pl.semaphore_signal(barrier, inc=1, device_id=peer, device_id_type=MESH)

    def gather_small(src, dst, send, recv):
        cps = [pltpu.make_async_remote_copy(src, dst.at[j], send.at[j], recv.at[j], device_id=peer, device_id_type=MESH)
               for j, peer in enumerate(peers)]
        for cp in cps:
            cp.start()
        return cps

    def row_sums(sq):
        part = sq[:, 0:128]
        for j in range(1, width // 128):
            part = part + sq[:, j * 128:(j + 1) * 128]
        t = jnp.sum(part.T, axis=0, keepdims=True)
        return jnp.broadcast_to(t, (8, tok))

    def as_row(ref):
        v = ref[...].astype(F32)
        return jnp.concatenate([v[j:j + 1, :] for j in range(width // 128)], axis=1)

    small[0].wait()
    hf = hid[...].astype(F32)
    sqs[...] = row_sums(hf * hf)
    pl.semaphore_wait(barrier, 4)
    sq_cps = gather_small(sqs, sqr, ss_sem, sr_sem)

    small[1].wait()
    expert_id = lax.broadcasted_iota(jnp.int32, (experts, tok), 0)
    chv = ch[...]
    hot = jnp.zeros((experts, tok), F32)
    for k in range(top_k):
        hot = hot + jnp.where(chv[k:k + 1, :] == expert_id, 1.0, 0.0)
    t0 = lax.broadcasted_iota(jnp.int32, (tok, tok), 0)
    t1 = lax.broadcasted_iota(jnp.int32, (tok, tok), 1)
    upper = jnp.where(t0 < t1, 1.0, 0.0).astype(BF16)
    before = jnp.dot(hot.astype(BF16), upper, preferred_element_type=F32)
    key_val = jnp.where((hot > 0.5) & (before < cap - 0.5), before, -1.0)
    dn = (((0,), (0,)), ((), ()))
    slot = lax.broadcasted_iota(jnp.int32, (cap, tok), 0).astype(F32)
    for e in range(experts):
        sel[e * cap:(e + 1) * cap, :] = jnp.where(key_val[e:e + 1, :] == slot, 1.0, 0.0).astype(BF16)

    filled = jnp.broadcast_to(jnp.minimum(jnp.sum(hot, axis=1, keepdims=True), float(cap)), (experts, 128))
    e0 = lax.broadcasted_iota(jnp.int32, (experts, experts), 0)
    e1 = lax.broadcasted_iota(jnp.int32, (experts, experts), 1)
    lower = jnp.where(e1 < e0, 1.0, 0.0).astype(BF16)
    start = jnp.dot(lower, filled.astype(BF16), preferred_element_type=F32)
    lane = lax.broadcasted_iota(jnp.int32, (cap, 128), 1).astype(F32)
    shift = jnp.zeros((1, 128), F32)
    for g in range(groups):
        base = float(max(0, rows * (g - half)))
        shift = jnp.maximum(shift, base - start[g * GE:g * GE + 1, :])
        for k in range(GE):
            e = g * GE + k
            pos = jnp.where(slot < filled[e:e + 1, :], slot + (start[e:e + 1, :] + shift), -1.0) - lane
            for j in range(half * rows // 128):
                dis[e * cap:(e + 1) * cap, j * 128:(j + 1) * 128] = jnp.where(pos == float(j * 128), 1.0, 0.0).astype(BF16)

    for cp in sq_cps:
        cp.wait_recv()
    tot = (sqs[0:1, :] + sqr[0, 0:1, :]) + (sqr[1, 0:1, :] + sqr[2, 0:1, :])
    inv = lax.rsqrt(tot / model_width + EPS)
    inv = jnp.broadcast_to(inv, (tok, tok)).T
    inv = jnp.concatenate([inv] * (width // 128), axis=1)
    b = (hf * inv * as_row(pre_ref)).astype(BF16)
    small[2].wait()
    lgs[...] = lax.dot_general(wr[...], b, (((1,), (1,)), ((), ())), preferred_element_type=F32)
    lg_cps = gather_small(lgs, lgr, ls_sem, lr_sem)
    for r in range(0, experts * cap, 256):
        xs[r:r + 256, :] = jnp.dot(sel[r:r + 256, :], b, preferred_element_type=F32).astype(BF16)
    mix[...] = jnp.zeros_like(mix)

    def gates():
        for cp in lg_cps:
            cp.wait_recv()
        lg = (lgs[...] + lgr[0]) + (lgr[1] + lgr[2])
        lg = lg - jnp.max(lg, axis=0, keepdims=True)
        ex = jnp.exp(lg)
        prob = ex / jnp.sum(ex, axis=0, keepdims=True)
        for e in range(experts):
            picked = jnp.where(key_val[e:e + 1, :] == slot, prob[e:e + 1, :], 0.0)
            gate[e * cap:(e + 1) * cap, :] = jnp.broadcast_to(jnp.sum(picked, axis=1, keepdims=True), (cap, 128))

    def send_z(i):
        return pltpu.make_async_remote_copy(zc.at[i, oc], rza.at[i], as_sem.at[i], ar_sem.at[i],
                                            device_id=mate, device_id_type=MESH)

    def send_s(i):
        return pltpu.make_async_remote_copy(zc.at[i, c, ox], rzb.at[i], bs_sem.at[i], br_sem.at[i],
                                            device_id=across, device_id_type=MESH)

    def g_copy(i, a, b, send, recv, peer):
        ref = gbuf.at[i, a, b]
        return pltpu.make_async_remote_copy(ref, ref, send.at[i], recv.at[i], device_id=peer, device_id_type=MESH)

    def send_g(i):
        return (g_copy(i, c, x, gcs_sem, gcr_sem, mate), g_copy(i, c, x, gxs_sem, gxr_sem, across))

    def recv_mate(i):
        return g_copy(i, oc, x, gcs_sem, gcr_sem, mate)

    def recv_across(i):
        return g_copy(i, c, ox, gxs_sem, gxr_sem, across)

    def forward_g(i):
        return g_copy(i, c, ox, gfs_sem, gfr_sem, mate)

    def recv_forward(i):
        return g_copy(i, oc, ox, gfs_sem, gfr_sem, mate)

    def stage_a(p, g):
        s = g % NR
        for cp in weight_copies(p, g):
            cp.wait()
        for k in range(GE):
            r = (g * GE + k) * cap
            xe = xs[r:r + cap, :]
            zs[r:r + cap, 0:fw] = jnp.dot(xe, wg[s, k], preferred_element_type=F32).astype(BF16)
            zs[r:r + cap, fw:2 * fw] = jnp.dot(xe, wu[s, k], preferred_element_type=F32).astype(BF16)

    def compact(i, k):
        depth = rows * (half + 1 + k)
        z = lax.dot_general(dis[0:depth, k * rows:(k + 1) * rows], zs[0:depth, :], dn,
                            preferred_element_type=F32).astype(BF16)
        for q in range(4):
            zc[i, q // 2, q % 2] = z[q * quarter:(q + 1) * quarter]
        send_z(i).start()

    def stage_b(i):
        send_z(i).wait_recv()
        zc[i, c, ox] = (zc[i, c, ox].astype(F32) + rza[i, ox].astype(F32)).astype(BF16)
        send_s(i).start()

    def stage_c(i):
        send_s(i).wait_recv()
        z = (zc[i, c, x].astype(F32) + rza[i, x].astype(F32) + rzb[i].astype(F32)).astype(BF16).astype(F32)
        act = jax.nn.gelu(z[:, 0:fw], approximate=True) * z[:, fw:2 * fw]
        gbuf[i, c, x] = act.astype(BF16)
        for cp in send_g(i):
            cp.start()

    def stage_d(i):
        recv_across(i).wait_recv()
        forward_g(i).start()

    def arrived(i):
        recv_mate(i).wait_recv()
        recv_forward(i).wait_recv()

    def stage_e(g):
        down_copy(g).wait()
        nblk = min(g + 1, half)
        depth = nblk * rows
        d = dis[g * rows:(g + 1) * rows, 0:depth]
        gs = [jnp.dot(d, gbuf[p * half:p * half + nblk].reshape(depth, fw), preferred_element_type=F32).astype(BF16)
              for p in range(NP)]
        gs = jnp.concatenate(gs, axis=1)
        us = []
        for k in range(GE):
            r = (g * GE + k) * cap
            y = jnp.dot(gs[k * cap:(k + 1) * cap], wd[g, k], preferred_element_type=F32).astype(BF16).astype(F32)
            gk = gate[r:r + cap, :]
            us.append((y * jnp.concatenate([gk] * (width // 128), axis=1)).astype(BF16))
        u = jnp.concatenate(us, axis=0)
        mix[...] += lax.dot_general(sel[g * rows:(g + 1) * rows, :], u, dn, preferred_element_type=F32)

    @pl.loop(0, NP)
    def _(p):
        first = p * half
        prev = first - half
        later = p > 0
        for g in range(groups):
            stage_a(p, g)
            if g < NR:
                for cp in weight_copies(p, g + NR):
                    cp.start()
            else:
                @pl.when(p == 0)
                def _():
                    for cp in weight_copies(1, g - NR):
                        cp.start()

                @pl.when(p == NP - 1)
                def _():
                    for h in (2 * (g - NR) + 1, 2 * (g - NR) + 2):
                        if h < groups:
                            down_copy(h).start()
            if g >= half:
                compact(first + g - half, g - half)
            if g > half:
                stage_b(first + g - half - 1)

            @pl.when(later)
            def _():
                if g == 0:
                    stage_b(prev + 3)
                    stage_c(prev)
                if g == 1:
                    gates()
                    stage_c(prev + 1)
                if g == 3:
                    stage_c(prev + 2)
                if g == 5:
                    stage_c(prev + 3)
                if g >= 4:
                    stage_d(prev + g - 4)

    last = (NP - 1) * half
    stage_b(last + 3)
    stage_c(last)
    stage_c(last + 1)
    for i in range(last):
        arrived(i)
    stage_d(last)
    stage_c(last + 2)
    arrived(last)
    stage_e(0)
    stage_d(last + 1)
    stage_c(last + 3)
    arrived(last + 1)
    stage_e(1)
    stage_d(last + 2)
    arrived(last + 2)
    stage_e(2)
    stage_d(last + 3)
    arrived(last + 3)
    for g in range(3, groups):
        stage_e(g)

    mcp = pltpu.make_async_remote_copy(mix, rmix, ms_sem, mr_sem, device_id=other, device_id_type=MESH)
    mcp.start()

    for i in range(NP * half):
        send_z(i).wait_send()
        send_s(i).wait_send()
        for cp in send_g(i):
            cp.wait_send()
        forward_g(i).wait_send()
    for cp in sq_cps + lg_cps:
        cp.wait_send()
    mcp.wait()
    m = mix[...] + rmix[...]
    sqs2[...] = row_sums(m * m)
    cps = gather_small(sqs2, sqr2, ps_sem, pr_sem)
    for cp in cps:
        cp.wait()
    tot = (sqs2[0:1, :] + sqr2[0, 0:1, :]) + (sqr2[1, 0:1, :] + sqr2[2, 0:1, :])
    inv = lax.rsqrt(tot / model_width + EPS)
    inv = jnp.broadcast_to(inv, (tok, tok)).T
    inv = jnp.concatenate([inv] * (width // 128), axis=1)
    out_ref[...] = (hid[...].astype(F32) + m * inv * as_row(post_ref)).astype(BF16)


def solution(mesh):
    emb_size = mesh.shape["emb"]

    def local_block(hidden, norm_pre, norm_post, w_router, w_gate, w_up, w_down, choice):
        tok, width = hidden.shape
        experts, _, wid = w_gate.shape
        top_k = choice.shape[1]
        cap = 2 * tok * top_k // experts
        groups = experts // GE
        nblk = NP * groups // 2
        slots, quarter, fw = experts * cap, GE * cap // 4, wid // NP
        dma = pltpu.SemaphoreType.DMA
        vmem = pltpu.VMEM
        assert emb_size == 4 and wid == width and slots == 2 * tok * top_k
        hbm = pl.BlockSpec(memory_space=pl.ANY)
        vm = pl.BlockSpec(memory_space=pltpu.VMEM)
        return pl.pallas_call(
            functools.partial(kernel, tok, wid, experts, cap, width, top_k, width * emb_size),
            out_shape=jax.ShapeDtypeStruct((tok, width), BF16),
            in_specs=[hbm, vm, vm, hbm, hbm, hbm, hbm, hbm],
            out_specs=vm,
            scratch_shapes=[
                vmem((tok, width), BF16), vmem((experts, width), BF16), vmem((top_k, tok), jnp.int32),
                vmem((NR, GE, width, fw), BF16), vmem((NR, GE, width, fw), BF16), vmem((groups, GE, wid, width), BF16),
                vmem((slots, width), BF16), vmem((slots, tok), BF16), vmem((slots, slots // 2), BF16), vmem((slots, 128), F32),
                vmem((slots, 2 * fw), BF16), vmem((nblk, 2, 2, quarter, 2 * fw), BF16), vmem((nblk, 2, quarter, 2 * fw), BF16),
                vmem((nblk, quarter, 2 * fw), BF16),
                vmem((nblk, 2, 2, quarter, fw), BF16),
                vmem((tok, width), F32), vmem((tok, width), F32),
                vmem((8, tok), F32), vmem((3, 8, tok), F32),
                vmem((experts, tok), F32), vmem((3, experts, tok), F32),
                vmem((8, tok), F32), vmem((3, 8, tok), F32),
                dma((3,)), dma((NR,)), dma((NR,)), dma((groups,)),
            ] + [dma((nblk,))] * 10 + [dma((3,))] * 6 + [dma, dma],
            compiler_params=pltpu.CompilerParams(
                collective_id=0, has_side_effects=True, vmem_limit_bytes=67043328),
        )(hidden, norm_pre.reshape(width // 128, 128), norm_post.reshape(width // 128, 128), w_router.T, w_gate, w_up, w_down, choice.T)

    in_specs = (P("dp", "emb"), P("emb"), P("emb"), P("emb", None), P(None, "emb", "ffn"), P(None, "emb", "ffn"), P(None, "ffn", "emb"), P("dp", None))
    return jax.shard_map(local_block, mesh=mesh, in_specs=in_specs, out_specs=P("dp", "emb"), check_vma=False)
```

time: 69.8 us -> 61 us (0.87)
  Pallas kernels: 68.1 us -> 59.3 us
    pallas_call x1, Pallas kernels: 68.1 us -> 59.3 us  [local_block(): pl.pallas_call(functools.partial(kernel, tok, wid, experts, cap, width, t...]
where the time goes in v2:
time: 61 us; the launch traced here: 60.8 us
  Pallas kernels  59.3 us (97%)
  local copies, waits for them, and re-layouts  1.57 us (3%)
    pallas_call x1, Pallas kernels, local_block(): pl.pallas_call(functools.partial(kernel, tok, wid, experts, cap, width, t...  59.3 us
    unnamed x1, local copies, waits for them, and re-layouts  1.57 us

profile of v2, /device:TPU:0, one launch (start us, length us, event | category | flops | bytes accessed | tf_op | source)
XLA Modules:
  0.0 60.8 jit_solution(17201771100801697299)
XLA Ops:
  0.0 59.3 %shard_map.82 = bf16[128,512]{1,0:T(8,128)(2,1)} custom-call(bf16[128,512]{1,0:T(8,128)(2,1)} %hid_hbm.1, bf16[4,128]{1,0:T(4,128)(2,1)} %bitcast.6, bf16[4,128]{1,0:T(4,128)(2,1)} %bitcast.7, bf16[64,512]{1,0:T(8,128)(2,1)} %bitcast.4, bf16[64,512,512]{2,1,0:T(8,128)(2,1)} %wg_hbm.1, bf16[64,512,512]{2,1,0:T(8,128)(2,1)} %wu_hbm.1, ...), custom_call_target="tpu_custom_call" | custom-call | tf_op jit(solution)/shard_map/pallas_call | solution.py:333
  59.3 1.6 %copy.10 = bf16[128,512]{1,0:T(8,128)(2,1)} copy(bf16[128,512]{1,0:T(8,128)(2,1)} %shard_map.82) | data formatting | bytes 262144

commit v3 on v2

--- a/solution.py
+++ b/solution.py
@@ -14,12 +14,12 @@
 
 GE = 8
 NP = 2
-NR = 4
+NR = 3
 
 
 def kernel(tok, wid, experts, cap, width, top_k, model_width,
            hid_hbm, pre_ref, post_ref, wr_hbm, wg_hbm, wu_hbm, wd_hbm, ch_hbm, out_ref,
-           hid, wr, ch, wg, wu, wd, xs, sel, dis, gate, zs, zc, rza, rzb, gbuf, mix, rmix,
+           hid, wr, ch, wg, wu, wd, xs, sel, dis, gate, zs, zc, rza, rzb, gbuf, y0, mix, rmix,
            sqs, sqr, lgs, lgr, sqs2, sqr2,
            small_sem, wg_sem, wu_sem, wd_sem,
            as_sem, ar_sem, bs_sem, br_sem, gcs_sem, gcr_sem, gxs_sem, gxr_sem, gfs_sem, gfr_sem,
@@ -41,8 +41,8 @@
 
     def weight_copies(p, g):
         e = pl.ds(g * GE, GE)
-        col = pl.ds(p * fw, fw) if isinstance(p, int) else pl.ds(pl.multiple_of(p * fw, fw), fw)
-        s = g % NR
+        col = pl.ds(p * fw, fw)
+        s = (p * groups + g) % NR
         return (pltpu.make_async_copy(wg_hbm.at[e, :, col], wg.at[s], wg_sem.at[s]),
                 pltpu.make_async_copy(wu_hbm.at[e, :, col], wu.at[s], wu_sem.at[s]))
 
@@ -54,11 +54,6 @@
              pltpu.make_async_copy(wr_hbm, wr, small_sem.at[2]))
     for cp in small:
         cp.start()
-    for g in range(NR):
-        for cp in weight_copies(0, g):
-            cp.start()
-    down_copy(0).start()
-
     barrier = pltpu.get_barrier_semaphore()
     for peer in peers + (other,):
         pl.semaphore_signal(barrier, inc=1, device_id=peer, device_id_type=MESH)
@@ -81,13 +76,18 @@
         v = ref[...].astype(F32)
         return jnp.concatenate([v[j:j + 1, :] for j in range(width // 128)], axis=1)
 
-    small[0].wait()
+    for cp in small:
+        cp.wait()
+    for g in range(NR):
+        for cp in weight_copies(0, g):
+            cp.start()
+    down_copy(0).start()
+    down_copy(1).start()
     hf = hid[...].astype(F32)
     sqs[...] = row_sums(hf * hf)
     pl.semaphore_wait(barrier, 4)
     sq_cps = gather_small(sqs, sqr, ss_sem, sr_sem)
 
-    small[1].wait()
     expert_id = lax.broadcasted_iota(jnp.int32, (experts, tok), 0)
     chv = ch[...]
     hot = jnp.zeros((experts, tok), F32)
@@ -126,16 +126,16 @@
     inv = jnp.broadcast_to(inv, (tok, tok)).T
     inv = jnp.concatenate([inv] * (width // 128), axis=1)
     b = (hf * inv * as_row(pre_ref)).astype(BF16)
-    small[2].wait()
     lgs[...] = lax.dot_general(wr[...], b, (((1,), (1,)), ((), ())), preferred_element_type=F32)
     lg_cps = gather_small(lgs, lgr, ls_sem, lr_sem)
-    for r in range(0, experts * cap, 256):
-        xs[r:r + 256, :] = jnp.dot(sel[r:r + 256, :], b, preferred_element_type=F32).astype(BF16)
+    def dispatch(g):
+        r = g * rows
+        xs[r:r + rows, :] = jnp.dot(sel[r:r + rows, :], b, preferred_element_type=F32).astype(BF16)
+
+    dispatch(0)
     mix[...] = jnp.zeros_like(mix)
 
     def gates():
-        for cp in lg_cps:
-            cp.wait_recv()
         lg = (lgs[...] + lgr[0]) + (lgr[1] + lgr[2])
         lg = lg - jnp.max(lg, axis=0, keepdims=True)
         ex = jnp.exp(lg)
@@ -172,126 +172,151 @@
         return g_copy(i, oc, ox, gfs_sem, gfr_sem, mate)
 
     def stage_a(p, g):
-        s = g % NR
-        for cp in weight_copies(p, g):
-            cp.wait()
+        s = (p * groups + g) % NR
         for k in range(GE):
             r = (g * GE + k) * cap
             xe = xs[r:r + cap, :]
             zs[r:r + cap, 0:fw] = jnp.dot(xe, wg[s, k], preferred_element_type=F32).astype(BF16)
             zs[r:r + cap, fw:2 * fw] = jnp.dot(xe, wu[s, k], preferred_element_type=F32).astype(BF16)
 
-    def compact(i, k):
-        depth = rows * (half + 1 + k)
-        z = lax.dot_general(dis[0:depth, k * rows:(k + 1) * rows], zs[0:depth, :], dn,
+    def compact(i):
+        k = i % half
+        lo, hi = k * rows, (k + half + 1) * rows
+        z = lax.dot_general(dis[lo:hi, k * rows:(k + 1) * rows], zs[lo:hi, :], dn,
                             preferred_element_type=F32).astype(BF16)
         for q in range(4):
             zc[i, q // 2, q % 2] = z[q * quarter:(q + 1) * quarter]
         send_z(i).start()
 
     def stage_b(i):
-        send_z(i).wait_recv()
         zc[i, c, ox] = (zc[i, c, ox].astype(F32) + rza[i, ox].astype(F32)).astype(BF16)
         send_s(i).start()
 
     def stage_c(i):
-        send_s(i).wait_recv()
         z = (zc[i, c, x].astype(F32) + rza[i, x].astype(F32) + rzb[i].astype(F32)).astype(BF16).astype(F32)
         act = jax.nn.gelu(z[:, 0:fw], approximate=True) * z[:, fw:2 * fw]
         gbuf[i, c, x] = act.astype(BF16)
         for cp in send_g(i):
             cp.start()
 
-    def stage_d(i):
-        recv_across(i).wait_recv()
-        forward_g(i).start()
+    def exchange(b_list, c_list, d_list):
+        for i in b_list:
+            send_z(i).wait_recv()
+        for i in c_list:
+            send_s(i).wait_recv()
+        for i in d_list:
+            recv_across(i).wait_recv()
+        for i in b_list:
+            stage_b(i)
+        for i in c_list:
+            stage_c(i)
+        for i in d_list:
+            forward_g(i).start()
 
     def arrived(i):
         recv_mate(i).wait_recv()
         recv_forward(i).wait_recv()
 
-    def stage_e(g):
-        down_copy(g).wait()
-        nblk = min(g + 1, half)
-        depth = nblk * rows
-        d = dis[g * rows:(g + 1) * rows, 0:depth]
-        gs = [jnp.dot(d, gbuf[p * half:p * half + nblk].reshape(depth, fw), preferred_element_type=F32).astype(BF16)
-              for p in range(NP)]
-        gs = jnp.concatenate(gs, axis=1)
+    def undo(p, g):
+        lo, hi = max(0, g - half), min(g + 1, half)
+        act = gbuf[p * half + lo:p * half + hi].reshape((hi - lo) * rows, fw)
+        return jnp.dot(dis[g * rows:(g + 1) * rows, lo * rows:hi * rows], act, preferred_element_type=F32).astype(BF16)
+
+    def down_first(g):
+        gs = undo(0, g)
+        for k in range(GE):
+            r = (g * GE + k) * cap
+            y0[r:r + cap, :] = jnp.dot(gs[k * cap:(k + 1) * cap], wd[g, k, 0:fw, :], preferred_element_type=F32)
+
+    def down_last(g, h, gs):
+        cols = slice(h * hw, (h + 1) * hw)
         us = []
         for k in range(GE):
             r = (g * GE + k) * cap
-            y = jnp.dot(gs[k * cap:(k + 1) * cap], wd[g, k], preferred_element_type=F32).astype(BF16).astype(F32)
+            y = y0[r:r + cap, cols] + jnp.dot(gs[k * cap:(k + 1) * cap], wd[g, k, fw:2 * fw, cols], preferred_element_type=F32)
             gk = gate[r:r + cap, :]
-            us.append((y * jnp.concatenate([gk] * (width // 128), axis=1)).astype(BF16))
+            us.append((y.astype(BF16).astype(F32) * jnp.concatenate([gk] * (hw // 128), axis=1)).astype(BF16))
         u = jnp.concatenate(us, axis=0)
-        mix[...] += lax.dot_general(sel[g * rows:(g + 1) * rows, :], u, dn, preferred_element_type=F32)
-
-    @pl.loop(0, NP)
-    def _(p):
-        first = p * half
-        prev = first - half
-        later = p > 0
-        for g in range(groups):
-            stage_a(p, g)
-            if g < NR:
-                for cp in weight_copies(p, g + NR):
-                    cp.start()
-            else:
-                @pl.when(p == 0)
-                def _():
-                    for cp in weight_copies(1, g - NR):
-                        cp.start()
-
-                @pl.when(p == NP - 1)
-                def _():
-                    for h in (2 * (g - NR) + 1, 2 * (g - NR) + 2):
-                        if h < groups:
-                            down_copy(h).start()
-            if g >= half:
-                compact(first + g - half, g - half)
-            if g > half:
-                stage_b(first + g - half - 1)
-
-            @pl.when(later)
-            def _():
-                if g == 0:
-                    stage_b(prev + 3)
-                    stage_c(prev)
-                if g == 1:
-                    gates()
-                    stage_c(prev + 1)
-                if g == 3:
-                    stage_c(prev + 2)
-                if g == 5:
-                    stage_c(prev + 3)
-                if g >= 4:
-                    stage_d(prev + g - 4)
-
-    last = (NP - 1) * half
-    stage_b(last + 3)
-    stage_c(last)
-    stage_c(last + 1)
-    for i in range(last):
-        arrived(i)
-    stage_d(last)
-    stage_c(last + 2)
-    arrived(last)
-    stage_e(0)
-    stage_d(last + 1)
-    stage_c(last + 3)
-    arrived(last + 1)
-    stage_e(1)
-    stage_d(last + 2)
-    arrived(last + 2)
-    stage_e(2)
-    stage_d(last + 3)
-    arrived(last + 3)
-    for g in range(3, groups):
-        stage_e(g)
-
-    mcp = pltpu.make_async_remote_copy(mix, rmix, ms_sem, mr_sem, device_id=other, device_id_type=MESH)
-    mcp.start()
+        mix[h] += lax.dot_general(sel[g * rows:(g + 1) * rows, :], u, dn, preferred_element_type=F32)
+
+    def down_both(g):
+        gs = undo(1, g)
+        for h in range(2):
+            down_last(g, h, gs)
+
+    hw = width // 2
+    b_at, c_at, d_at = {7: (0,), 8: (1,), 9: (2,), 10: (3,), 14: (4,), 15: (5,)}, {10: (0,), 11: (1,), 12: (2,), 13: (3,)}, {14: (0,), 15: (1,)}
+    for t in range(NP * groups):
+        p, g = divmod(t, groups)
+        for cp in weight_copies(p, g):
+            cp.wait()
+        if t == 3:
+            for cp in lg_cps:
+                cp.wait_recv()
+        exchange(b_at.get(t, ()), c_at.get(t, ()), d_at.get(t, ()))
+        if g > half:
+            compact(p * half + g - half - 1)
+        elif g == 0 and p > 0:
+            compact(p * half - 1)
+        stage_a(p, g)
+        if p == 0 and g + 1 < groups:
+            dispatch(g + 1)
+        if t == 3:
+            gates()
+        if t + NR < NP * groups:
+            for cp in weight_copies(*divmod(t + NR, groups)):
+                cp.start()
+        elif t + NR < NP * groups + 2:
+            down_copy(t + NR - NP * groups + 2).start()
+        else:
+            for h in range(4, groups):
+                down_copy(h).start()
+
+    exchange((6,), (), (2, 3))
+    compact(7)
+    down_copy(0).wait()
+    arrived(0)
+    down_first(0)
+    exchange((7,), (4,), ())
+    arrived(1)
+    arrived(2)
+    down_copy(1).wait()
+    down_copy(2).wait()
+    down_first(1)
+    down_first(2)
+    exchange((), (5,), ())
+    arrived(3)
+    down_copy(3).wait()
+    down_first(3)
+    exchange((), (6,), ())
+    down_copy(4).wait()
+    down_first(4)
+    exchange((), (7,), ())
+    down_copy(5).wait()
+    down_first(5)
+    exchange((), (), (4,))
+    exchange((), (), (5,))
+    down_copy(6).wait()
+    down_first(6)
+    exchange((), (), (6,))
+    arrived(4)
+    down_both(0)
+    exchange((), (), (7,))
+    arrived(5)
+    down_both(1)
+    down_copy(7).wait()
+    down_first(7)
+    arrived(6)
+    down_both(2)
+    arrived(7)
+    for h in range(2):
+        for g in range(3, groups):
+            r = g * rows
+            if h == 0:
+                zs[r:r + rows, 0:fw] = undo(1, g)
+            down_last(g, h, zs[r:r + rows, 0:fw])
+        pltpu.make_async_remote_copy(mix.at[h], rmix.at[h], ms_sem.at[h], mr_sem.at[h],
+                                     device_id=other, device_id_type=MESH).start()
 
     for i in range(NP * half):
         send_z(i).wait_send()
@@ -301,8 +326,12 @@
         forward_g(i).wait_send()
     for cp in sq_cps + lg_cps:
         cp.wait_send()
-    mcp.wait()
-    m = mix[...] + rmix[...]
+    ms = []
+    for h in range(2):
+        pltpu.make_async_remote_copy(mix.at[h], rmix.at[h], ms_sem.at[h], mr_sem.at[h],
+                                     device_id=other, device_id_type=MESH).wait()
+        ms.append(mix[h] + rmix[h])
+    m = jnp.concatenate(ms, axis=1)
     sqs2[...] = row_sums(m * m)
     cps = gather_small(sqs2, sqr2, ps_sem, pr_sem)
     for cp in cps:
@@ -342,12 +371,12 @@
                 vmem((slots, 2 * fw), BF16), vmem((nblk, 2, 2, quarter, 2 * fw), BF16), vmem((nblk, 2, quarter, 2 * fw), BF16),
                 vmem((nblk, quarter, 2 * fw), BF16),
                 vmem((nblk, 2, 2, quarter, fw), BF16),
-                vmem((tok, width), F32), vmem((tok, width), F32),
+                vmem((slots, width), F32), vmem((2, tok, width // 2), F32), vmem((2, tok, width // 2), F32),
                 vmem((8, tok), F32), vmem((3, 8, tok), F32),
                 vmem((experts, tok), F32), vmem((3, experts, tok), F32),
                 vmem((8, tok), F32), vmem((3, 8, tok), F32),
                 dma((3,)), dma((NR,)), dma((NR,)), dma((groups,)),
-            ] + [dma((nblk,))] * 10 + [dma((3,))] * 6 + [dma, dma],
+            ] + [dma((nblk,))] * 10 + [dma((3,))] * 6 + [dma((2,))] * 2,
             compiler_params=pltpu.CompilerParams(
                 collective_id=0, has_side_effects=True, vmem_limit_bytes=67043328),
         )(hidden, norm_pre.reshape(width // 128, 128), norm_post.reshape(width // 128, 128), w_router.T, w_gate, w_up, w_down, choice.T)

time: 61 us -> 59.9 us (0.982)
  Pallas kernels: 59.3 us -> 58.2 us
    pallas_call x1, Pallas kernels: 59.3 us -> 58.2 us  [local_block(): pl.pallas_call(functools.partial(kernel, tok, wid, experts, cap, width, t...]
where the time goes in v3:
time: 59.9 us; the launch traced here: 59.7 us
  Pallas kernels  58.2 us (97%)
  local copies, waits for them, and re-layouts  1.57 us (3%)
    pallas_call x1, Pallas kernels, local_block(): pl.pallas_call(functools.partial(kernel, tok, wid, experts, cap, width, t...  58.2 us
    unnamed x1, local copies, waits for them, and re-layouts  1.57 us

profile of v3, /device:TPU:0, one launch (start us, length us, event | category | flops | bytes accessed | tf_op | source)
XLA Modules:
  0.0 59.7 jit_solution(2487674462083359034)
XLA Ops:
  0.0 58.2 %shard_map.82 = bf16[128,512]{1,0:T(8,128)(2,1)} custom-call(bf16[128,512]{1,0:T(8,128)(2,1)} %hid_hbm.1, bf16[4,128]{1,0:T(4,128)(2,1)} %bitcast.6, bf16[4,128]{1,0:T(4,128)(2,1)} %bitcast.7, bf16[64,512]{1,0:T(8,128)(2,1)} %bitcast.4, bf16[64,512,512]{2,1,0:T(8,128)(2,1)} %wg_hbm.1, bf16[64,512,512]{2,1,0:T(8,128)(2,1)} %wu_hbm.1, ...), custom_call_target="tpu_custom_call" | custom-call | tf_op jit(solution)/shard_map/pallas_call | solution.py:362
  58.2 1.6 %copy.10 = bf16[128,512]{1,0:T(8,128)(2,1)} copy(bf16[128,512]{1,0:T(8,128)(2,1)} %shard_map.82) | data formatting | bytes 262144

commit v4 on v3

--- a/solution.py
+++ b/solution.py
@@ -15,18 +15,20 @@
 GE = 8
 NP = 2
 NR = 3
+WIN = 48
 
 
 def kernel(tok, wid, experts, cap, width, top_k, model_width,
            hid_hbm, pre_ref, post_ref, wr_hbm, wg_hbm, wu_hbm, wd_hbm, ch_hbm, out_ref,
-           hid, wr, ch, wg, wu, wd, xs, sel, dis, gate, zs, zc, rza, rzb, gbuf, y0, mix, rmix,
+           hid, wr, ch, wg, wu, wd, xs, sel, dis, keyw, probs, selw, gate, posv, poss, zs, zc, rza, rzb, gbuf, act, mix, rmix,
            sqs, sqr, lgs, lgr, sqs2, sqr2,
-           small_sem, wg_sem, wu_sem, wd_sem,
+           small_sem, pos_sem, wg_sem, wu_sem, wd_sem,
            as_sem, ar_sem, bs_sem, br_sem, gcs_sem, gcr_sem, gxs_sem, gxr_sem, gfs_sem, gfr_sem,
            ss_sem, sr_sem, ls_sem, lr_sem, ps_sem, pr_sem, ms_sem, mr_sem):
     groups = experts // GE
     half = groups // 2
     rows = GE * cap
+    slots = experts * cap
     quarter = rows // 4
     fw = wid // NP
     emb = lax.axis_index("emb")
@@ -110,14 +112,18 @@
     start = jnp.dot(lower, filled.astype(BF16), preferred_element_type=F32)
     lane = lax.broadcasted_iota(jnp.int32, (cap, 128), 1).astype(F32)
     shift = jnp.zeros((1, 128), F32)
+    place = []
     for g in range(groups):
         base = float(max(0, rows * (g - half)))
         shift = jnp.maximum(shift, base - start[g * GE:g * GE + 1, :])
-        for k in range(GE):
-            e = g * GE + k
-            pos = jnp.where(slot < filled[e:e + 1, :], slot + (start[e:e + 1, :] + shift), -1.0) - lane
-            for j in range(half * rows // 128):
-                dis[e * cap:(e + 1) * cap, j * 128:(j + 1) * 128] = jnp.where(pos == float(j * 128), 1.0, 0.0).astype(BF16)
+        place.append(start[g * GE:(g + 1) * GE, :] + shift)
+    place = jnp.concatenate(place, axis=0)
+    for e in range(experts):
+        pos = jnp.where(slot < filled[e:e + 1, :], slot + place[e:e + 1, :], -1.0) - lane
+        for j in range(half * rows // 128):
+            dis[e * cap:(e + 1) * cap, j * 128:(j + 1) * 128] = jnp.where(pos == float(j * 128), 1.0, 0.0).astype(BF16)
+    whole = place.astype(jnp.int32)
+    keyw[...] = jnp.where(key_val >= 0.0, key_val + (whole & 15).astype(F32), -1.0)
 
     for cp in sq_cps:
         cp.wait_recv()
@@ -135,14 +141,38 @@
     dispatch(0)
     mix[...] = jnp.zeros_like(mix)
 
-    def gates():
+    pos_cp = pltpu.make_async_copy(posv, poss, pos_sem)
+
+    def window_starts():
+        ids = jnp.concatenate([ch[...]] * (tok // top_k), axis=0).T
+        expert = lax.broadcasted_iota(jnp.int32, (tok, tok), 1)
+        at = lax.broadcasted_iota(jnp.int32, (tok, tok), 0)
+        num = jnp.zeros((tok, tok), jnp.int32)
+        for k in range(top_k):
+            num = num + jnp.where(ids[:, k:k + 1] == expert, 1, 0)
+        num = jnp.minimum(jnp.sum(num, axis=0, keepdims=True), cap)
+        num = jnp.broadcast_to(num, (tok, tok)).T
+        off = jnp.sum(jnp.where(at < expert, num, 0), axis=0, keepdims=True)
+        base = jnp.maximum(expert[0:1, :] // GE - half, 0) * rows - off
+        base = jnp.broadcast_to(base, (tok, tok)).T
+        pos = off + jnp.max(jnp.where(at <= expert, base, -slots), axis=0, keepdims=True)
+        pos = jnp.minimum(pos, half * rows)
+        posv[...] = jnp.broadcast_to(pos >> 4, (8, tok))
+        pos_cp.start()
+
+    def softmax():
         lg = (lgs[...] + lgr[0]) + (lgr[1] + lgr[2])
         lg = lg - jnp.max(lg, axis=0, keepdims=True)
         ex = jnp.exp(lg)
-        prob = ex / jnp.sum(ex, axis=0, keepdims=True)
-        for e in range(experts):
-            picked = jnp.where(key_val[e:e + 1, :] == slot, prob[e:e + 1, :], 0.0)
-            gate[e * cap:(e + 1) * cap, :] = jnp.broadcast_to(jnp.sum(picked, axis=1, keepdims=True), (cap, 128))
+        probs[...] = ex / jnp.sum(ex, axis=0, keepdims=True)
+
+    def windows(g):
+        w = lax.broadcasted_iota(jnp.int32, (WIN, tok), 0).astype(F32)
+        for e in range(g * GE, (g + 1) * GE):
+            hit = keyw[e:e + 1, :] == w
+            selw[e * WIN:(e + 1) * WIN, :] = jnp.where(hit, 1.0, 0.0).astype(BF16)
+            picked = jnp.sum(jnp.where(hit, probs[e:e + 1, :], 0.0), axis=1, keepdims=True)
+            gate[e * WIN:(e + 1) * WIN, :] = jnp.broadcast_to(picked, (WIN, 128))
 
     def send_z(i):
         return pltpu.make_async_remote_copy(zc.at[i, oc], rza.at[i], as_sem.at[i], ar_sem.at[i],
@@ -153,7 +183,8 @@
                                             device_id=across, device_id_type=MESH)
 
     def g_copy(i, a, b, send, recv, peer):
-        ref = gbuf.at[i, a, b]
+        row = (i % half) * rows + (2 * a + b) * quarter
+        ref = gbuf.at[i // half, pl.ds(pl.multiple_of(row, quarter), quarter), :]
         return pltpu.make_async_remote_copy(ref, ref, send.at[i], recv.at[i], device_id=peer, device_id_type=MESH)
 
     def send_g(i):
@@ -194,8 +225,9 @@
 
     def stage_c(i):
         z = (zc[i, c, x].astype(F32) + rza[i, x].astype(F32) + rzb[i].astype(F32)).astype(BF16).astype(F32)
-        act = jax.nn.gelu(z[:, 0:fw], approximate=True) * z[:, fw:2 * fw]
-        gbuf[i, c, x] = act.astype(BF16)
+        prod = jax.nn.gelu(z[:, 0:fw], approximate=True) * z[:, fw:2 * fw]
+        row = (i % half) * rows + (2 * c + x) * quarter
+        gbuf[i // half, pl.ds(pl.multiple_of(row, quarter), quarter), :] = prod.astype(BF16)
         for cp in send_g(i):
             cp.start()
 
@@ -216,36 +248,28 @@
     def arrived(i):
         recv_mate(i).wait_recv()
         recv_forward(i).wait_recv()
-
-    def undo(p, g):
-        lo, hi = max(0, g - half), min(g + 1, half)
-        act = gbuf[p * half + lo:p * half + hi].reshape((hi - lo) * rows, fw)
-        return jnp.dot(dis[g * rows:(g + 1) * rows, lo * rows:hi * rows], act, preferred_element_type=F32).astype(BF16)
-
-    def down_first(g):
-        gs = undo(0, g)
-        for k in range(GE):
-            r = (g * GE + k) * cap
-            y0[r:r + cap, :] = jnp.dot(gs[k * cap:(k + 1) * cap], wd[g, k, 0:fw, :], preferred_element_type=F32)
-
-    def down_last(g, h, gs):
+        p, r = i // half, (i % half) * rows
+        act[r // 16:(r + rows) // 16, :, p * fw:(p + 1) * fw] = gbuf[p, r:r + rows, :].reshape(rows // 16, 16, fw)
+
+    def down(g, h):
         cols = slice(h * hw, (h + 1) * hw)
         us = []
         for k in range(GE):
-            r = (g * GE + k) * cap
-            y = y0[r:r + cap, cols] + jnp.dot(gs[k * cap:(k + 1) * cap], wd[g, k, fw:2 * fw, cols], preferred_element_type=F32)
-            gk = gate[r:r + cap, :]
-            us.append((y.astype(BF16).astype(F32) * jnp.concatenate([gk] * (hw // 128), axis=1)).astype(BF16))
+            e = g * GE + k
+            at = poss[0, e]
+            win = jnp.concatenate([act[at + j] for j in range(WIN // 16)], axis=0)
+            y = jnp.dot(win, wd[g, k, :, cols], preferred_element_type=F32)
+            gk = gate[e * WIN:(e + 1) * WIN, :]
+            gk = jnp.concatenate([gk] * (hw // 128), axis=1)
+            us.append(jnp.where(gk > 0.0, y.astype(BF16).astype(F32) * gk, 0.0).astype(BF16))
         u = jnp.concatenate(us, axis=0)
-        mix[h] += lax.dot_general(sel[g * rows:(g + 1) * rows, :], u, dn, preferred_element_type=F32)
-
-    def down_both(g):
-        gs = undo(1, g)
-        for h in range(2):
-            down_last(g, h, gs)
+        r = g * GE * WIN
+        mix[h] += lax.dot_general(selw[r:r + GE * WIN, :], u, dn, preferred_element_type=F32)
 
     hw = width // 2
-    b_at, c_at, d_at = {7: (0,), 8: (1,), 9: (2,), 10: (3,), 14: (4,), 15: (5,)}, {10: (0,), 11: (1,), 12: (2,), 13: (3,)}, {14: (0,), 15: (1,)}
+    b_at = {6: (0,), 7: (1,), 8: (2,), 9: (3,), 14: (4,), 15: (5,)}
+    c_at = {10: (0,), 11: (1,), 12: (2,), 14: (3,)}
+    d_at = {14: (0,), 15: (1,)}
     for t in range(NP * groups):
         p, g = divmod(t, groups)
         for cp in weight_copies(p, g):
@@ -261,8 +285,12 @@
         stage_a(p, g)
         if p == 0 and g + 1 < groups:
             dispatch(g + 1)
+        if t == 2:
+            window_starts()
         if t == 3:
-            gates()
+            softmax()
+        if 4 <= t < 4 + groups:
+            windows(t - 4)
         if t + NR < NP * groups:
             for cp in weight_copies(*divmod(t + NR, groups)):
                 cp.start()
@@ -272,49 +300,37 @@
             for h in range(4, groups):
                 down_copy(h).start()
 
-    exchange((6,), (), (2, 3))
+    exchange((6,), (), (2,))
     compact(7)
+    pos_cp.wait()
+    exchange((), (4,), (3,))
+    exchange((7,), (), ())
+    for i in range(half):
+        arrived(i)
+    exchange((), (5,), ())
+    exchange((), (6,), (4,))
+    exchange((), (7,), ())
+    exchange((), (), (5,))
+    arrived(4)
     down_copy(0).wait()
-    arrived(0)
-    down_first(0)
-    exchange((7,), (4,), ())
-    arrived(1)
-    arrived(2)
+    down(0, 0)
+    exchange((), (), (6,))
+    down(0, 1)
+    arrived(5)
     down_copy(1).wait()
+    down(1, 0)
+    exchange((), (), (7,))
+    down(1, 1)
+    arrived(6)
     down_copy(2).wait()
-    down_first(1)
-    down_first(2)
-    exchange((), (5,), ())
-    arrived(3)
-    down_copy(3).wait()
-    down_first(3)
-    exchange((), (6,), ())
-    down_copy(4).wait()
-    down_first(4)
-    exchange((), (7,), ())
-    down_copy(5).wait()
-    down_first(5)
-    exchange((), (), (4,))
-    exchange((), (), (5,))
-    down_copy(6).wait()
-    down_first(6)
-    exchange((), (), (6,))
-    arrived(4)
-    down_both(0)
-    exchange((), (), (7,))
-    arrived(5)
-    down_both(1)
-    down_copy(7).wait()
-    down_first(7)
-    arrived(6)
-    down_both(2)
+    down(2, 0)
+    down(2, 1)
+    for g in range(3, groups):
+        down_copy(g).wait()
     arrived(7)
     for h in range(2):
         for g in range(3, groups):
-            r = g * rows
-            if h == 0:
-                zs[r:r + rows, 0:fw] = undo(1, g)
-            down_last(g, h, zs[r:r + rows, 0:fw])
+            down(g, h)
         pltpu.make_async_remote_copy(mix.at[h], rmix.at[h], ms_sem.at[h], mr_sem.at[h],
                                      device_id=other, device_id_type=MESH).start()
 
@@ -356,7 +372,7 @@
         slots, quarter, fw = experts * cap, GE * cap // 4, wid // NP
         dma = pltpu.SemaphoreType.DMA
         vmem = pltpu.VMEM
-        assert emb_size == 4 and wid == width and slots == 2 * tok * top_k
+        assert emb_size == 4 and wid == width and slots == 2 * tok * top_k and WIN == cap + 16
         hbm = pl.BlockSpec(memory_space=pl.ANY)
         vm = pl.BlockSpec(memory_space=pltpu.VMEM)
         return pl.pallas_call(
@@ -367,15 +383,17 @@
             scratch_shapes=[
                 vmem((tok, width), BF16), vmem((experts, width), BF16), vmem((top_k, tok), jnp.int32),
                 vmem((NR, GE, width, fw), BF16), vmem((NR, GE, width, fw), BF16), vmem((groups, GE, wid, width), BF16),
-                vmem((slots, width), BF16), vmem((slots, tok), BF16), vmem((slots, slots // 2), BF16), vmem((slots, 128), F32),
+                vmem((slots, width), BF16), vmem((slots, tok), BF16), vmem((slots, slots // 2), BF16),
+                vmem((experts, tok), F32), vmem((experts, tok), F32), vmem((experts * WIN, tok), BF16), vmem((experts * WIN, 128), F32),
+                vmem((8, tok), jnp.int32), pltpu.SMEM((8, tok), jnp.int32),
                 vmem((slots, 2 * fw), BF16), vmem((nblk, 2, 2, quarter, 2 * fw), BF16), vmem((nblk, 2, quarter, 2 * fw), BF16),
                 vmem((nblk, quarter, 2 * fw), BF16),
-                vmem((nblk, 2, 2, quarter, fw), BF16),
-                vmem((slots, width), F32), vmem((2, tok, width // 2), F32), vmem((2, tok, width // 2), F32),
+                vmem((NP, slots // 2, fw), BF16), vmem(((slots // 2 + WIN) // 16, 16, wid), BF16),
+                vmem((2, tok, width // 2), F32), vmem((2, tok, width // 2), F32),
                 vmem((8, tok), F32), vmem((3, 8, tok), F32),
                 vmem((experts, tok), F32), vmem((3, experts, tok), F32),
                 vmem((8, tok), F32), vmem((3, 8, tok), F32),
-                dma((3,)), dma((NR,)), dma((NR,)), dma((groups,)),
+                dma((3,)), dma, dma((NR,)), dma((NR,)), dma((groups,)),
             ] + [dma((nblk,))] * 10 + [dma((3,))] * 6 + [dma((2,))] * 2,
             compiler_params=pltpu.CompilerParams(
                 collective_id=0, has_side_effects=True, vmem_limit_bytes=67043328),

time: 59.9 us -> 57.5 us (0.960)
  Pallas kernels: 58.2 us -> 55.8 us
    pallas_call x1, Pallas kernels: 58.2 us -> 55.8 us  [local_block(): pl.pallas_call(functools.partial(kernel, tok, wid, experts, cap, width, t...]
where the time goes in v4:
time: 57.5 us; the launch traced here: 57.4 us
  Pallas kernels  55.8 us (97%)
  local copies, waits for them, and re-layouts  1.57 us (3%)
    pallas_call x1, Pallas kernels, local_block(): pl.pallas_call(functools.partial(kernel, tok, wid, experts, cap, width, t...  55.8 us
    unnamed x1, local copies, waits for them, and re-layouts  1.57 us

profile of v4, /device:TPU:0, one launch (start us, length us, event | category | flops | bytes accessed | tf_op | source)
XLA Modules:
  0.0 57.4 jit_solution(10528703356929899661)
XLA Ops:
  0.0 55.8 %shard_map.82 = bf16[128,512]{1,0:T(8,128)(2,1)} custom-call(bf16[128,512]{1,0:T(8,128)(2,1)} %hid_hbm.1, bf16[4,128]{1,0:T(4,128)(2,1)} %bitcast.6, bf16[4,128]{1,0:T(4,128)(2,1)} %bitcast.7, bf16[64,512]{1,0:T(8,128)(2,1)} %bitcast.4, bf16[64,512,512]{2,1,0:T(8,128)(2,1)} %wg_hbm.1, bf16[64,512,512]{2,1,0:T(8,128)(2,1)} %wu_hbm.1, ...), custom_call_target="tpu_custom_call" | custom-call | tf_op jit(solution)/shard_map/pallas_call | solution.py:378
  55.8 1.6 %copy.10 = bf16[128,512]{1,0:T(8,128)(2,1)} copy(bf16[128,512]{1,0:T(8,128)(2,1)} %shard_map.82) | data formatting | bytes 262144

commit v5 on v4

--- a/solution.py
+++ b/solution.py
@@ -12,15 +12,16 @@
 F32 = jnp.float32
 BF16 = jnp.bfloat16
 
-GE = 8
-NP = 2
+GE = 16
+GD = 8
+NP = 4
 NR = 3
 WIN = 48
 
 
 def kernel(tok, wid, experts, cap, width, top_k, model_width,
            hid_hbm, pre_ref, post_ref, wr_hbm, wg_hbm, wu_hbm, wd_hbm, ch_hbm, out_ref,
-           hid, wr, ch, wg, wu, wd, xs, sel, dis, keyw, probs, selw, gate, posv, poss, zs, zc, rza, rzb, gbuf, act, mix, rmix,
+           hid, wr, ch, wgu, wd, xs, sel, dis, keyw, probs, selw, gate, posv, poss, zs, zc, rza, rzb, gbuf, act, mix, rmix,
            sqs, sqr, lgs, lgr, sqs2, sqr2,
            small_sem, pos_sem, wg_sem, wu_sem, wd_sem,
            as_sem, ar_sem, bs_sem, br_sem, gcs_sem, gcr_sem, gxs_sem, gxr_sem, gfs_sem, gfr_sem,
@@ -28,6 +29,7 @@
     groups = experts // GE
     half = groups // 2
     rows = GE * cap
+    downs = experts // GD
     slots = experts * cap
     quarter = rows // 4
     fw = wid // NP
@@ -45,11 +47,11 @@
         e = pl.ds(g * GE, GE)
         col = pl.ds(p * fw, fw)
         s = (p * groups + g) % NR
-        return (pltpu.make_async_copy(wg_hbm.at[e, :, col], wg.at[s], wg_sem.at[s]),
-                pltpu.make_async_copy(wu_hbm.at[e, :, col], wu.at[s], wu_sem.at[s]))
+        return (pltpu.make_async_copy(wg_hbm.at[e, :, col], wgu.at[s, :, :, 0:fw], wg_sem.at[s]),
+                pltpu.make_async_copy(wu_hbm.at[e, :, col], wgu.at[s, :, :, fw:2 * fw], wu_sem.at[s]))
 
     def down_copy(g):
-        return pltpu.make_async_copy(wd_hbm.at[pl.ds(g * GE, GE)], wd.at[g], wd_sem.at[g])
+        return pltpu.make_async_copy(wd_hbm.at[pl.ds(g * GD, GD)], wd.at[g], wd_sem.at[g])
 
     small = (pltpu.make_async_copy(hid_hbm, hid, small_sem.at[0]),
              pltpu.make_async_copy(ch_hbm, ch, small_sem.at[1]),
@@ -135,8 +137,8 @@
     lgs[...] = lax.dot_general(wr[...], b, (((1,), (1,)), ((), ())), preferred_element_type=F32)
     lg_cps = gather_small(lgs, lgr, ls_sem, lr_sem)
     def dispatch(g):
-        r = g * rows
-        xs[r:r + rows, :] = jnp.dot(sel[r:r + rows, :], b, preferred_element_type=F32).astype(BF16)
+        for r in range(g * rows, (g + 1) * rows, 256):
+            xs[r:r + 256, :] = jnp.dot(sel[r:r + 256, :], b, preferred_element_type=F32).astype(BF16)
 
     dispatch(0)
     mix[...] = jnp.zeros_like(mix)
@@ -168,7 +170,7 @@
 
     def windows(g):
         w = lax.broadcasted_iota(jnp.int32, (WIN, tok), 0).astype(F32)
-        for e in range(g * GE, (g + 1) * GE):
+        for e in range(g * GD, (g + 1) * GD):
             hit = keyw[e:e + 1, :] == w
             selw[e * WIN:(e + 1) * WIN, :] = jnp.where(hit, 1.0, 0.0).astype(BF16)
             picked = jnp.sum(jnp.where(hit, probs[e:e + 1, :], 0.0), axis=1, keepdims=True)
@@ -207,8 +209,7 @@
         for k in range(GE):
             r = (g * GE + k) * cap
             xe = xs[r:r + cap, :]
-            zs[r:r + cap, 0:fw] = jnp.dot(xe, wg[s, k], preferred_element_type=F32).astype(BF16)
-            zs[r:r + cap, fw:2 * fw] = jnp.dot(xe, wu[s, k], preferred_element_type=F32).astype(BF16)
+            zs[r:r + cap, :] = jnp.dot(xe, wgu[s, k], preferred_element_type=F32).astype(BF16)
 
     def compact(i):
         k = i % half
@@ -254,8 +255,8 @@
     def down(g, h):
         cols = slice(h * hw, (h + 1) * hw)
         us = []
-        for k in range(GE):
-            e = g * GE + k
+        for k in range(GD):
+            e = g * GD + k
             at = poss[0, e]
             win = jnp.concatenate([act[at + j] for j in range(WIN // 16)], axis=0)
             y = jnp.dot(win, wd[g, k, :, cols], preferred_element_type=F32)
@@ -263,13 +264,13 @@
             gk = jnp.concatenate([gk] * (hw // 128), axis=1)
             us.append(jnp.where(gk > 0.0, y.astype(BF16).astype(F32) * gk, 0.0).astype(BF16))
         u = jnp.concatenate(us, axis=0)
-        r = g * GE * WIN
-        mix[h] += lax.dot_general(selw[r:r + GE * WIN, :], u, dn, preferred_element_type=F32)
+        r = g * GD * WIN
+        mix[h] += lax.dot_general(selw[r:r + GD * WIN, :], u, dn, preferred_element_type=F32)
 
     hw = width // 2
-    b_at = {6: (0,), 7: (1,), 8: (2,), 9: (3,), 14: (4,), 15: (5,)}
-    c_at = {10: (0,), 11: (1,), 12: (2,), 14: (3,)}
-    d_at = {14: (0,), 15: (1,)}
+    b_at = {4: (0,), 5: (1,), 8: (2,), 9: (3,), 12: (4,), 13: (5,)}
+    c_at = {7: (0,), 8: (1,), 11: (2,), 12: (3,), 15: (4,)}
+    d_at = {10: (0,), 11: (1,), 14: (2,), 15: (3,)}
     for t in range(NP * groups):
         p, g = divmod(t, groups)
         for cp in weight_copies(p, g):
@@ -289,47 +290,39 @@
             window_starts()
         if t == 3:
             softmax()
-        if 4 <= t < 4 + groups:
+        if 4 <= t < 4 + downs:
             windows(t - 4)
         if t + NR < NP * groups:
             for cp in weight_copies(*divmod(t + NR, groups)):
                 cp.start()
-        elif t + NR < NP * groups + 2:
-            down_copy(t + NR - NP * groups + 2).start()
         else:
-            for h in range(4, groups):
+            n = t + NR - NP * groups
+            for h in range(2 + 2 * n, 4 + 2 * n):
                 down_copy(h).start()
 
-    exchange((6,), (), (2,))
+    exchange((6,), (), ())
     compact(7)
+    exchange((), (5,), (4,))
+    exchange((7,), (), ())
     pos_cp.wait()
-    exchange((), (4,), (3,))
-    exchange((7,), (), ())
-    for i in range(half):
+    for i in range(4):
         arrived(i)
-    exchange((), (5,), ())
-    exchange((), (6,), (4,))
+    for g in range(downs):
+        down_copy(g).wait()
+    exchange((), (6,), (5,))
+    arrived(4)
     exchange((), (7,), ())
-    exchange((), (), (5,))
-    arrived(4)
-    down_copy(0).wait()
+    arrived(5)
+    exchange((), (), (6,))
+    arrived(6)
     down(0, 0)
-    exchange((), (), (6,))
+    exchange((), (), (7,))
     down(0, 1)
-    arrived(5)
-    down_copy(1).wait()
     down(1, 0)
-    exchange((), (), (7,))
     down(1, 1)
-    arrived(6)
-    down_copy(2).wait()
-    down(2, 0)
-    down(2, 1)
-    for g in range(3, groups):
-        down_copy(g).wait()
     arrived(7)
     for h in range(2):
-        for g in range(3, groups):
+        for g in range(2, downs):
             down(g, h)
         pltpu.make_async_remote_copy(mix.at[h], rmix.at[h], ms_sem.at[h], mr_sem.at[h],
                                      device_id=other, device_id_type=MESH).start()
@@ -382,7 +375,7 @@
             out_specs=vm,
             scratch_shapes=[
                 vmem((tok, width), BF16), vmem((experts, width), BF16), vmem((top_k, tok), jnp.int32),
-                vmem((NR, GE, width, fw), BF16), vmem((NR, GE, width, fw), BF16), vmem((groups, GE, wid, width), BF16),
+                vmem((NR, GE, width, 2 * fw), BF16), vmem((experts // GD, GD, wid, width), BF16),
                 vmem((slots, width), BF16), vmem((slots, tok), BF16), vmem((slots, slots // 2), BF16),
                 vmem((experts, tok), F32), vmem((experts, tok), F32), vmem((experts * WIN, tok), BF16), vmem((experts * WIN, 128), F32),
                 vmem((8, tok), jnp.int32), pltpu.SMEM((8, tok), jnp.int32),
@@ -393,7 +386,7 @@
                 vmem((8, tok), F32), vmem((3, 8, tok), F32),
                 vmem((experts, tok), F32), vmem((3, experts, tok), F32),
                 vmem((8, tok), F32), vmem((3, 8, tok), F32),
-                dma((3,)), dma, dma((NR,)), dma((NR,)), dma((groups,)),
+                dma((3,)), dma, dma((NR,)), dma((NR,)), dma((experts // GD,)),
             ] + [dma((nblk,))] * 10 + [dma((3,))] * 6 + [dma((2,))] * 2,
             compiler_params=pltpu.CompilerParams(
                 collective_id=0, has_side_effects=True, vmem_limit_bytes=67043328),

time: 57.5 us -> 62.7 us (1.090)
  Pallas kernels: 55.8 us -> 61 us
    pallas_call x1, Pallas kernels: 55.8 us -> 61 us  [local_block(): pl.pallas_call(functools.partial(kernel, tok, wid, experts, cap, width, t...]
where the time goes in v5:
time: 62.7 us; the launch traced here: 62.5 us
  Pallas kernels  61 us (97%)
  local copies, waits for them, and re-layouts  1.57 us (3%)
    pallas_call x1, Pallas kernels, local_block(): pl.pallas_call(functools.partial(kernel, tok, wid, experts, cap, width, t...  61 us
    unnamed x1, local copies, waits for them, and re-layouts  1.57 us

profile of v5, /device:TPU:0, one launch (start us, length us, event | category | flops | bytes accessed | tf_op | source)
XLA Modules:
  0.0 62.5 jit_solution(9127446557514821804)
XLA Ops:
  0.0 61.0 %shard_map.82 = bf16[128,512]{1,0:T(8,128)(2,1)} custom-call(bf16[128,512]{1,0:T(8,128)(2,1)} %hid_hbm.1, bf16[4,128]{1,0:T(4,128)(2,1)} %bitcast.6, bf16[4,128]{1,0:T(4,128)(2,1)} %bitcast.7, bf16[64,512]{1,0:T(8,128)(2,1)} %bitcast.4, bf16[64,512,512]{2,1,0:T(8,128)(2,1)} %wg_hbm.1, bf16[64,512,512]{2,1,0:T(8,128)(2,1)} %wu_hbm.1, ...), custom_call_target="tpu_custom_call" | custom-call | tf_op jit(solution)/shard_map/pallas_call | solution.py:371
  61.0 1.6 %copy.10 = bf16[128,512]{1,0:T(8,128)(2,1)} copy(bf16[128,512]{1,0:T(8,128)(2,1)} %shard_map.82) | data formatting | bytes 262144

commit v6 on v4

--- a/solution.py
+++ b/solution.py
@@ -282,9 +282,9 @@
             compact(p * half + g - half - 1)
         elif g == 0 and p > 0:
             compact(p * half - 1)
-        stage_a(p, g)
         if p == 0 and g + 1 < groups:
             dispatch(g + 1)
+        stage_a(p, g)
         if t == 2:
             window_starts()
         if t == 3:
@@ -309,20 +309,18 @@
         arrived(i)
     exchange((), (5,), ())
     exchange((), (6,), (4,))
-    exchange((), (7,), ())
-    exchange((), (), (5,))
+    for g in range(3):
+        down_copy(g).wait()
+    exchange((), (7,), (5,))
     arrived(4)
-    down_copy(0).wait()
     down(0, 0)
+    down(0, 1)
     exchange((), (), (6,))
-    down(0, 1)
     arrived(5)
-    down_copy(1).wait()
     down(1, 0)
+    down(1, 1)
     exchange((), (), (7,))
-    down(1, 1)
     arrived(6)
-    down_copy(2).wait()
     down(2, 0)
     down(2, 1)
     for g in range(3, groups):
@@ -377,7 +375,7 @@
         vm = pl.BlockSpec(memory_space=pltpu.VMEM)
         return pl.pallas_call(
             functools.partial(kernel, tok, wid, experts, cap, width, top_k, width * emb_size),
-            out_shape=jax.ShapeDtypeStruct((tok, width), BF16),
+            out_shape=pltpu.VMEM((tok, width), BF16),
             in_specs=[hbm, vm, vm, hbm, hbm, hbm, hbm, hbm],
             out_specs=vm,
             scratch_shapes=[
@@ -396,7 +394,7 @@
                 dma((3,)), dma, dma((NR,)), dma((NR,)), dma((groups,)),
             ] + [dma((nblk,))] * 10 + [dma((3,))] * 6 + [dma((2,))] * 2,
             compiler_params=pltpu.CompilerParams(
-                collective_id=0, has_side_effects=True, vmem_limit_bytes=67043328),
+                collective_id=0, has_side_effects=True, vmem_limit_bytes=66600000),
         )(hidden, norm_pre.reshape(width // 128, 128), norm_post.reshape(width // 128, 128), w_router.T, w_gate, w_up, w_down, choice.T)
 
     in_specs = (P("dp", "emb"), P("emb"), P("emb"), P("emb", None), P(None, "emb", "ffn"), P(None, "emb", "ffn"), P(None, "ffn", "emb"), P("dp", None))

time: 57.5 us -> 56.6 us (0.984)
  local copies, waits for them, and re-layouts: 1.57 us -> 0.66 us
    unnamed x1, local copies, waits for them, and re-layouts: 1.57 us -> 0.66 us
where the time goes in v6:
time: 56.6 us; the launch traced here: 56.5 us
  Pallas kernels  55.9 us (99%)
  local copies, waits for them, and re-layouts  0.66 us (1%)
    pallas_call x1, Pallas kernels, local_block(): pl.pallas_call(functools.partial(kernel, tok, wid, experts, cap, width, t...  55.9 us

profile of v6, /device:TPU:0, one launch (start us, length us, event | category | flops | bytes accessed | tf_op | source)
XLA Modules:
  0.0 56.5 jit_solution(1420186868438832582)
XLA Ops:
  0.0 55.9 %shard_map.82 = bf16[128,512]{1,0:T(8,128)(2,1)S(1)} custom-call(bf16[128,512]{1,0:T(8,128)(2,1)} %hid_hbm.1, bf16[4,128]{1,0:T(4,128)(2,1)} %bitcast.6, bf16[4,128]{1,0:T(4,128)(2,1)} %bitcast.7, bf16[64,512]{1,0:T(8,128)(2,1)} %bitcast.4, bf16[64,512,512]{2,1,0:T(8,128)(2,1)} %wg_hbm.1, bf16[64,512,512]{2,1,0:T(8,128)(2,1)} %wu_hbm.1, ...), custom_call_target="tpu_custom_call" | custom-call | tf_op jit(solution)/shard_map/pallas_call | solution.py:376
  55.9 0.7 %copy.10 = bf16[128,512]{1,0:T(8,128)(2,1)} copy(bf16[128,512]{1,0:T(8,128)(2,1)S(1)} %shard_map.82) | data formatting | bytes 262144

commit v7 on v6

--- a/solution.py
+++ b/solution.py
@@ -23,7 +23,7 @@
            hid, wr, ch, wg, wu, wd, xs, sel, dis, keyw, probs, selw, gate, posv, poss, zs, zc, rza, rzb, gbuf, act, mix, rmix,
            sqs, sqr, lgs, lgr, sqs2, sqr2,
            small_sem, pos_sem, wg_sem, wu_sem, wd_sem,
-           as_sem, ar_sem, bs_sem, br_sem, gcs_sem, gcr_sem, gxs_sem, gxr_sem, gfs_sem, gfr_sem,
+           as_sem, ar_sem, bs_sem, br_sem, gs_sem, gcr_sem, gxr_sem,
            ss_sem, sr_sem, ls_sem, lr_sem, ps_sem, pr_sem, ms_sem, mr_sem):
     groups = experts // GE
     half = groups // 2
@@ -61,11 +61,11 @@
         pl.semaphore_signal(barrier, inc=1, device_id=peer, device_id_type=MESH)
 
     def gather_small(src, dst, send, recv):
-        cps = [pltpu.make_async_remote_copy(src, dst.at[j], send.at[j], recv.at[j], device_id=peer, device_id_type=MESH)
+        cps = [pltpu.make_async_remote_copy(src, dst.at[j], send, recv, device_id=peer, device_id_type=MESH)
                for j, peer in enumerate(peers)]
         for cp in cps:
             cp.start()
-        return cps
+        return pltpu.make_async_remote_copy(dst, dst, send, recv, device_id=mate, device_id_type=MESH)
 
     def row_sums(sq):
         part = sq[:, 0:128]
@@ -125,8 +125,7 @@
     whole = place.astype(jnp.int32)
     keyw[...] = jnp.where(key_val >= 0.0, key_val + (whole & 15).astype(F32), -1.0)
 
-    for cp in sq_cps:
-        cp.wait_recv()
+    sq_cps.wait_recv()
     tot = (sqs[0:1, :] + sqr[0, 0:1, :]) + (sqr[1, 0:1, :] + sqr[2, 0:1, :])
     inv = lax.rsqrt(tot / model_width + EPS)
     inv = jnp.broadcast_to(inv, (tok, tok)).T
@@ -175,32 +174,31 @@
             gate[e * WIN:(e + 1) * WIN, :] = jnp.broadcast_to(picked, (WIN, 128))
 
     def send_z(i):
-        return pltpu.make_async_remote_copy(zc.at[i, oc], rza.at[i], as_sem.at[i], ar_sem.at[i],
+        return pltpu.make_async_remote_copy(zc.at[i, oc], rza.at[i], as_sem, ar_sem.at[i],
                                             device_id=mate, device_id_type=MESH)
 
     def send_s(i):
-        return pltpu.make_async_remote_copy(zc.at[i, c, ox], rzb.at[i], bs_sem.at[i], br_sem.at[i],
+        return pltpu.make_async_remote_copy(zc.at[i, c, ox], rzb.at[i], bs_sem, br_sem.at[i],
                                             device_id=across, device_id_type=MESH)
 
-    def g_copy(i, a, b, send, recv, peer):
+    def g_copy(i, a, b, recv, peer):
         row = (i % half) * rows + (2 * a + b) * quarter
         ref = gbuf.at[i // half, pl.ds(pl.multiple_of(row, quarter), quarter), :]
-        return pltpu.make_async_remote_copy(ref, ref, send.at[i], recv.at[i], device_id=peer, device_id_type=MESH)
+        return pltpu.make_async_remote_copy(ref, ref, gs_sem, recv.at[i], device_id=peer, device_id_type=MESH)
 
     def send_g(i):
-        return (g_copy(i, c, x, gcs_sem, gcr_sem, mate), g_copy(i, c, x, gxs_sem, gxr_sem, across))
+        return (g_copy(i, c, x, gcr_sem, mate), g_copy(i, c, x, gxr_sem, across))
 
     def recv_mate(i):
-        return g_copy(i, oc, x, gcs_sem, gcr_sem, mate)
+        row = (i % half) * rows + 2 * oc * quarter
+        ref = gbuf.at[i // half, pl.ds(pl.multiple_of(row, 2 * quarter), 2 * quarter), :]
+        return pltpu.make_async_remote_copy(ref, ref, gs_sem, gcr_sem.at[i], device_id=mate, device_id_type=MESH)
 
     def recv_across(i):
-        return g_copy(i, c, ox, gxs_sem, gxr_sem, across)
+        return g_copy(i, c, ox, gxr_sem, across)
 
     def forward_g(i):
-        return g_copy(i, c, ox, gfs_sem, gfr_sem, mate)
-
-    def recv_forward(i):
-        return g_copy(i, oc, ox, gfs_sem, gfr_sem, mate)
+        return g_copy(i, c, ox, gcr_sem, mate)
 
     def stage_a(p, g):
         s = (p * groups + g) % NR
@@ -247,7 +245,6 @@
 
     def arrived(i):
         recv_mate(i).wait_recv()
-        recv_forward(i).wait_recv()
         p, r = i // half, (i % half) * rows
         act[r // 16:(r + rows) // 16, :, p * fw:(p + 1) * fw] = gbuf[p, r:r + rows, :].reshape(rows // 16, 16, fw)
 
@@ -275,8 +272,7 @@
         for cp in weight_copies(p, g):
             cp.wait()
         if t == 3:
-            for cp in lg_cps:
-                cp.wait_recv()
+            lg_cps.wait_recv()
         exchange(b_at.get(t, ()), c_at.get(t, ()), d_at.get(t, ()))
         if g > half:
             compact(p * half + g - half - 1)
@@ -332,14 +328,12 @@
         pltpu.make_async_remote_copy(mix.at[h], rmix.at[h], ms_sem.at[h], mr_sem.at[h],
                                      device_id=other, device_id_type=MESH).start()
 
-    for i in range(NP * half):
-        send_z(i).wait_send()
-        send_s(i).wait_send()
-        for cp in send_g(i):
-            cp.wait_send()
-        forward_g(i).wait_send()
-    for cp in sq_cps + lg_cps:
-        cp.wait_send()
+    pltpu.make_async_remote_copy(rza, rza, as_sem, ar_sem.at[0], device_id=mate, device_id_type=MESH).wait_send()
+    pltpu.make_async_remote_copy(rzb, rzb, bs_sem, br_sem.at[0], device_id=mate, device_id_type=MESH).wait_send()
+    sent = gbuf.at[:, 0:3 * rows, :]
+    pltpu.make_async_remote_copy(sent, sent, gs_sem, gcr_sem.at[0], device_id=mate, device_id_type=MESH).wait_send()
+    sq_cps.wait_send()
+    lg_cps.wait_send()
     ms = []
     for h in range(2):
         pltpu.make_async_remote_copy(mix.at[h], rmix.at[h], ms_sem.at[h], mr_sem.at[h],
@@ -347,9 +341,7 @@
         ms.append(mix[h] + rmix[h])
     m = jnp.concatenate(ms, axis=1)
     sqs2[...] = row_sums(m * m)
-    cps = gather_small(sqs2, sqr2, ps_sem, pr_sem)
-    for cp in cps:
-        cp.wait()
+    gather_small(sqs2, sqr2, ps_sem, pr_sem).wait()
     tot = (sqs2[0:1, :] + sqr2[0, 0:1, :]) + (sqr2[1, 0:1, :] + sqr2[2, 0:1, :])
     inv = lax.rsqrt(tot / model_width + EPS)
     inv = jnp.broadcast_to(inv, (tok, tok)).T
@@ -392,7 +384,7 @@
                 vmem((experts, tok), F32), vmem((3, experts, tok), F32),
                 vmem((8, tok), F32), vmem((3, 8, tok), F32),
                 dma((3,)), dma, dma((NR,)), dma((NR,)), dma((groups,)),
-            ] + [dma((nblk,))] * 10 + [dma((3,))] * 6 + [dma((2,))] * 2,
+            ] + [dma, dma((nblk,))] * 2 + [dma, dma((nblk,)), dma((nblk,))] + [dma] * 6 + [dma((2,))] * 2,
             compiler_params=pltpu.CompilerParams(
                 collective_id=0, has_side_effects=True, vmem_limit_bytes=66600000),
         )(hidden, norm_pre.reshape(width // 128, 128), norm_post.reshape(width // 128, 128), w_router.T, w_gate, w_up, w_down, choice.T)

time: 56.6 us -> 56.1 us (level)
  Pallas kernels: 55.9 us -> 55.3 us
where the time goes in v7:
time: 56.1 us; the launch traced here: 56 us
  Pallas kernels  55.3 us (99%)
  local copies, waits for them, and re-layouts  0.66 us (1%)
    pallas_call x1, Pallas kernels, local_block(): pl.pallas_call(functools.partial(kernel, tok, wid, experts, cap, width, t...  55.3 us

profile of v7, /device:TPU:0, one launch (start us, length us, event | category | flops | bytes accessed | tf_op | source)
XLA Modules:
  0.0 56.0 jit_solution(13946076083407885416)
XLA Ops:
  0.0 55.3 %shard_map.82 = bf16[128,512]{1,0:T(8,128)(2,1)S(1)} custom-call(bf16[128,512]{1,0:T(8,128)(2,1)} %hid_hbm.1, bf16[4,128]{1,0:T(4,128)(2,1)} %bitcast.6, bf16[4,128]{1,0:T(4,128)(2,1)} %bitcast.7, bf16[64,512]{1,0:T(8,128)(2,1)} %bitcast.4, bf16[64,512,512]{2,1,0:T(8,128)(2,1)} %wg_hbm.1, bf16[64,512,512]{2,1,0:T(8,128)(2,1)} %wu_hbm.1, ...), custom_call_target="tpu_custom_call" | custom-call | tf_op jit(solution)/shard_map/pallas_call | solution.py:368
  55.4 0.7 %copy.10 = bf16[128,512]{1,0:T(8,128)(2,1)} copy(bf16[128,512]{1,0:T(8,128)(2,1)S(1)} %shard_map.82) | data formatting | bytes 262144

commit v8 on v7

--- a/solution.py
+++ b/solution.py
@@ -20,11 +20,11 @@
 
 def kernel(tok, wid, experts, cap, width, top_k, model_width,
            hid_hbm, pre_ref, post_ref, wr_hbm, wg_hbm, wu_hbm, wd_hbm, ch_hbm, out_ref,
-           hid, wr, ch, wg, wu, wd, xs, sel, dis, keyw, probs, selw, gate, posv, poss, zs, zc, rza, rzb, gbuf, act, mix, rmix,
+           hid, wr, ch, wg, wu, wd, xs, sel, dis, keyw, probs, selw, gate, posv, poss, zs, zc, rza, rzb, gbuf, act, mix, rmix, total,
            sqs, sqr, lgs, lgr, sqs2, sqr2,
            small_sem, pos_sem, wg_sem, wu_sem, wd_sem,
            as_sem, ar_sem, bs_sem, br_sem, gs_sem, gcr_sem, gxr_sem,
-           ss_sem, sr_sem, ls_sem, lr_sem, ps_sem, pr_sem, ms_sem, mr_sem):
+           ss_sem, sr_sem, ls_sem, lr_sem, ps_sem, pr_sem, ms_sem, mr_sem, ts_sem, tr_sem):
     groups = experts // GE
     half = groups // 2
     rows = GE * cap
@@ -40,6 +40,8 @@
     diag = {"emb": ox * 2 + oc}
     other = {"ffn": 1 - ffn}
     peers = (mate, across, diag)
+    fo = 1 - ffn
+    everyone = peers + (other,) + tuple({"emb": peer["emb"], "ffn": fo} for peer in peers)
 
     def weight_copies(p, g):
         e = pl.ds(g * GE, GE)
@@ -57,10 +59,10 @@
     for cp in small:
         cp.start()
     barrier = pltpu.get_barrier_semaphore()
-    for peer in peers + (other,):
+    for peer in everyone:
         pl.semaphore_signal(barrier, inc=1, device_id=peer, device_id_type=MESH)
 
-    def gather_small(src, dst, send, recv):
+    def gather_small(src, dst, send, recv, peers=peers):
         cps = [pltpu.make_async_remote_copy(src, dst.at[j], send, recv, device_id=peer, device_id_type=MESH)
                for j, peer in enumerate(peers)]
         for cp in cps:
@@ -87,7 +89,7 @@
     down_copy(1).start()
     hf = hid[...].astype(F32)
     sqs[...] = row_sums(hf * hf)
-    pl.semaphore_wait(barrier, 4)
+    pl.semaphore_wait(barrier, 7)
     sq_cps = gather_small(sqs, sqr, ss_sem, sr_sem)
 
     expert_id = lax.broadcasted_iota(jnp.int32, (experts, tok), 0)
@@ -261,7 +263,7 @@
             us.append(jnp.where(gk > 0.0, y.astype(BF16).astype(F32) * gk, 0.0).astype(BF16))
         u = jnp.concatenate(us, axis=0)
         r = g * GE * WIN
-        mix[h] += lax.dot_general(selw[r:r + GE * WIN, :], u, dn, preferred_element_type=F32)
+        mix[h] += lax.dot_general(selw[r:r + GE * WIN, :], u, dn, preferred_element_type=F32).reshape(2, tok // 2, hw)
 
     hw = width // 2
     b_at = {6: (0,), 7: (1,), 8: (2,), 9: (3,), 14: (4,), 15: (5,)}
@@ -322,11 +324,18 @@
     for g in range(3, groups):
         down_copy(g).wait()
     arrived(7)
+    def send_half(h):
+        return pltpu.make_async_remote_copy(mix.at[h, fo], rmix.at[h], ms_sem.at[h], mr_sem.at[h],
+                                            device_id=other, device_id_type=MESH)
+
+    def send_sum(h, part):
+        ref = total.at[h, part]
+        return pltpu.make_async_remote_copy(ref, ref, ts_sem.at[h], tr_sem.at[h], device_id=other, device_id_type=MESH)
+
     for h in range(2):
         for g in range(3, groups):
             down(g, h)
-        pltpu.make_async_remote_copy(mix.at[h], rmix.at[h], ms_sem.at[h], mr_sem.at[h],
-                                     device_id=other, device_id_type=MESH).start()
+        send_half(h).start()
 
     pltpu.make_async_remote_copy(rza, rza, as_sem, ar_sem.at[0], device_id=mate, device_id_type=MESH).wait_send()
     pltpu.make_async_remote_copy(rzb, rzb, bs_sem, br_sem.at[0], device_id=mate, device_id_type=MESH).wait_send()
@@ -334,15 +343,26 @@
     pltpu.make_async_remote_copy(sent, sent, gs_sem, gcr_sem.at[0], device_id=mate, device_id_type=MESH).wait_send()
     sq_cps.wait_send()
     lg_cps.wait_send()
-    ms = []
+    own = []
     for h in range(2):
-        pltpu.make_async_remote_copy(mix.at[h], rmix.at[h], ms_sem.at[h], mr_sem.at[h],
-                                     device_id=other, device_id_type=MESH).wait()
-        ms.append(mix[h] + rmix[h])
-    m = jnp.concatenate(ms, axis=1)
-    sqs2[...] = row_sums(m * m)
-    gather_small(sqs2, sqr2, ps_sem, pr_sem).wait()
-    tot = (sqs2[0:1, :] + sqr2[0, 0:1, :]) + (sqr2[1, 0:1, :] + sqr2[2, 0:1, :])
+        send_half(h).wait()
+        own.append(mix[h, ffn] + rmix[h])
+        total[h, ffn] = own[h]
+        if h == 0:
+            send_sum(0, ffn).start()
+    own = jnp.concatenate(own, axis=1)
+    sq = own * own
+    sqs2[...] = row_sums(jnp.concatenate([sq, sq], axis=0))
+    last_cps = gather_small(sqs2, sqr2, ps_sem, pr_sem, everyone)
+    send_sum(1, ffn).start()
+    last_cps.wait()
+    mine = (sqs2[0:1, :] + sqr2[0, 0:1, :]) + (sqr2[1, 0:1, :] + sqr2[2, 0:1, :])
+    theirs = (sqr2[3, 0:1, :] + sqr2[4, 0:1, :]) + (sqr2[5, 0:1, :] + sqr2[6, 0:1, :])
+    tot = jnp.where(lax.broadcasted_iota(jnp.int32, (1, tok), 1) // (tok // 2) == ffn, mine, theirs)
+    for h in range(2):
+        send_sum(h, ffn).wait_send()
+        send_sum(h, fo).wait_recv()
+    m = jnp.concatenate([total[h].reshape(tok, hw) for h in range(2)], axis=1)
     inv = lax.rsqrt(tot / model_width + EPS)
     inv = jnp.broadcast_to(inv, (tok, tok)).T
     inv = jnp.concatenate([inv] * (width // 128), axis=1)
@@ -379,12 +399,12 @@
                 vmem((slots, 2 * fw), BF16), vmem((nblk, 2, 2, quarter, 2 * fw), BF16), vmem((nblk, 2, quarter, 2 * fw), BF16),
                 vmem((nblk, quarter, 2 * fw), BF16),
                 vmem((NP, slots // 2, fw), BF16), vmem(((slots // 2 + WIN) // 16, 16, wid), BF16),
-                vmem((2, tok, width // 2), F32), vmem((2, tok, width // 2), F32),
+                vmem((2, 2, tok // 2, width // 2), F32), vmem((2, tok // 2, width // 2), F32), vmem((2, 2, tok // 2, width // 2), F32),
                 vmem((8, tok), F32), vmem((3, 8, tok), F32),
                 vmem((experts, tok), F32), vmem((3, experts, tok), F32),
-                vmem((8, tok), F32), vmem((3, 8, tok), F32),
+                vmem((8, tok), F32), vmem((7, 8, tok), F32),
                 dma((3,)), dma, dma((NR,)), dma((NR,)), dma((groups,)),
-            ] + [dma, dma((nblk,))] * 2 + [dma, dma((nblk,)), dma((nblk,))] + [dma] * 6 + [dma((2,))] * 2,
+            ] + [dma, dma((nblk,))] * 2 + [dma, dma((nblk,)), dma((nblk,))] + [dma] * 6 + [dma((2,))] * 4,
             compiler_params=pltpu.CompilerParams(
                 collective_id=0, has_side_effects=True, vmem_limit_bytes=66600000),
         )(hidden, norm_pre.reshape(width // 128, 128), norm_post.reshape(width // 128, 128), w_router.T, w_gate, w_up, w_down, choice.T)

time: 56.1 us -> 54.8 us (0.977)
  Pallas kernels: 55.3 us -> 54 us
    pallas_call x1, Pallas kernels: 55.3 us -> 54 us  [local_block(): pl.pallas_call(functools.partial(kernel, tok, wid, experts, cap, width, t...]
where the time goes in v8:
time: 54.8 us; the launch traced here: 54.7 us
  Pallas kernels  54 us (99%)
  local copies, waits for them, and re-layouts  0.66 us (1%)
    pallas_call x1, Pallas kernels, local_block(): pl.pallas_call(functools.partial(kernel, tok, wid, experts, cap, width, t...  54 us

profile of v8, /device:TPU:0, one launch (start us, length us, event | category | flops | bytes accessed | tf_op | source)
XLA Modules:
  0.0 54.7 jit_solution(11231557153048898158)
XLA Ops:
  0.0 54.0 %shard_map.82 = bf16[128,512]{1,0:T(8,128)(2,1)S(1)} custom-call(bf16[128,512]{1,0:T(8,128)(2,1)} %hid_hbm.1, bf16[4,128]{1,0:T(4,128)(2,1)} %bitcast.6, bf16[4,128]{1,0:T(4,128)(2,1)} %bitcast.7, bf16[64,512]{1,0:T(8,128)(2,1)} %bitcast.4, bf16[64,512,512]{2,1,0:T(8,128)(2,1)} %wg_hbm.1, bf16[64,512,512]{2,1,0:T(8,128)(2,1)} %wu_hbm.1, ...), custom_call_target="tpu_custom_call" | custom-call | tf_op jit(solution)/shard_map/pallas_call | solution.py:388
  54.0 0.7 %copy.10 = bf16[128,512]{1,0:T(8,128)(2,1)} copy(bf16[128,512]{1,0:T(8,128)(2,1)S(1)} %shard_map.82) | data formatting | bytes 262144

commit v9 on v8

--- a/solution.py
+++ b/solution.py
@@ -273,7 +273,7 @@
         p, g = divmod(t, groups)
         for cp in weight_copies(p, g):
             cp.wait()
-        if t == 3:
+        if t == 8:
             lg_cps.wait_recv()
         exchange(b_at.get(t, ()), c_at.get(t, ()), d_at.get(t, ()))
         if g > half:
@@ -283,12 +283,12 @@
         if p == 0 and g + 1 < groups:
             dispatch(g + 1)
         stage_a(p, g)
-        if t == 2:
+        if t == 8:
+            softmax()
+        if t == 9:
             window_starts()
-        if t == 3:
-            softmax()
-        if 4 <= t < 4 + groups:
-            windows(t - 4)
+        if 8 <= t < 8 + groups:
+            windows(t - 8)
         if t + NR < NP * groups:
             for cp in weight_copies(*divmod(t + NR, groups)):
                 cp.start()

time: 54.8 us -> 54.9 us (level)
  no operation moved by 1% of the time
where the time goes in v9:
time: 54.9 us; the launch traced here: 54.7 us
  Pallas kernels  54.1 us (99%)
  local copies, waits for them, and re-layouts  0.66 us (1%)
    pallas_call x1, Pallas kernels, local_block(): pl.pallas_call(functools.partial(kernel, tok, wid, experts, cap, width, t...  54.1 us

profile of v9, /device:TPU:0, one launch (start us, length us, event | category | flops | bytes accessed | tf_op | source)
XLA Modules:
  0.0 54.7 jit_solution(18163775121715259797)
XLA Ops:
  0.0 54.1 %shard_map.82 = bf16[128,512]{1,0:T(8,128)(2,1)S(1)} custom-call(bf16[128,512]{1,0:T(8,128)(2,1)} %hid_hbm.1, bf16[4,128]{1,0:T(4,128)(2,1)} %bitcast.6, bf16[4,128]{1,0:T(4,128)(2,1)} %bitcast.7, bf16[64,512]{1,0:T(8,128)(2,1)} %bitcast.4, bf16[64,512,512]{2,1,0:T(8,128)(2,1)} %wg_hbm.1, bf16[64,512,512]{2,1,0:T(8,128)(2,1)} %wu_hbm.1, ...), custom_call_target="tpu_custom_call" | custom-call | tf_op jit(solution)/shard_map/pallas_call | solution.py:388
  54.1 0.7 %copy.10 = bf16[128,512]{1,0:T(8,128)(2,1)} copy(bf16[128,512]{1,0:T(8,128)(2,1)S(1)} %shard_map.82) | data formatting | bytes 262144

commit v10 on v9

--- a/solution.py
+++ b/solution.py
@@ -285,10 +285,11 @@
         stage_a(p, g)
         if t == 8:
             softmax()
-        if t == 9:
+        if t == 11:
             window_starts()
-        if 8 <= t < 8 + groups:
-            windows(t - 8)
+        if 9 <= t < 9 + groups // 2:
+            windows(2 * (t - 9))
+            windows(2 * (t - 9) + 1)
         if t + NR < NP * groups:
             for cp in weight_copies(*divmod(t + NR, groups)):
                 cp.start()
@@ -301,8 +302,8 @@
     exchange((6,), (), (2,))
     compact(7)
     pos_cp.wait()
+    exchange((7,), (), ())
     exchange((), (4,), (3,))
-    exchange((7,), (), ())
     for i in range(half):
         arrived(i)
     exchange((), (5,), ())

time: 54.9 us -> 55.5 us (1.011)
  Pallas kernels: 54.1 us -> 54.7 us
    pallas_call x1, Pallas kernels: 54.1 us -> 54.7 us  [local_block(): pl.pallas_call(functools.partial(kernel, tok, wid, experts, cap, width, t...]
where the time goes in v10:
time: 55.5 us; the launch traced here: 55.4 us
  Pallas kernels  54.7 us (99%)
  local copies, waits for them, and re-layouts  0.66 us (1%)
    pallas_call x1, Pallas kernels, local_block(): pl.pallas_call(functools.partial(kernel, tok, wid, experts, cap, width, t...  54.7 us

profile of v10, /device:TPU:0, one launch (start us, length us, event | category | flops | bytes accessed | tf_op | source)
XLA Modules:
  0.0 55.4 jit_solution(7195164218748178092)
XLA Ops:
  0.0 54.7 %shard_map.82 = bf16[128,512]{1,0:T(8,128)(2,1)S(1)} custom-call(bf16[128,512]{1,0:T(8,128)(2,1)} %hid_hbm.1, bf16[4,128]{1,0:T(4,128)(2,1)} %bitcast.6, bf16[4,128]{1,0:T(4,128)(2,1)} %bitcast.7, bf16[64,512]{1,0:T(8,128)(2,1)} %bitcast.4, bf16[64,512,512]{2,1,0:T(8,128)(2,1)} %wg_hbm.1, bf16[64,512,512]{2,1,0:T(8,128)(2,1)} %wu_hbm.1, ...), custom_call_target="tpu_custom_call" | custom-call | tf_op jit(solution)/shard_map/pallas_call | solution.py:389
  54.7 0.7 %copy.10 = bf16[128,512]{1,0:T(8,128)(2,1)} copy(bf16[128,512]{1,0:T(8,128)(2,1)S(1)} %shard_map.82) | data formatting | bytes 262144
